TPU v7x, 16 devices: a 4x2x1 block of a 4x4x8 slice. The times are simulated.
16 devices in a mesh: rep: 2 (over y, z), dp: 8 (over x, core).
Axes of the slice: x: 4, y: 2, z: 1, core: 2. Of those that a mesh axis runs over, the one named last changes fastest.
The devices are a block of a 4x4x8 slice.
Arguments:
- hidden: bfloat16 [1024, 2048], P(('rep', 'dp')), parts along dimension 0
- ckv_cache: bfloat16 [1024, 256, 512], P(('rep', 'dp')), parts along dimension 0
- kr_cache: bfloat16 [1024, 256, 64], P(('rep', 'dp')), parts along dimension 0
- seq_lens: int32 [1024], P(('rep', 'dp')), parts along dimension 0
- expert_ids: int32 [1024, 6], P(('rep', 'dp')), parts along dimension 0
- attn_gain: bfloat16 [2048], replicated
- kv_gain: bfloat16 [512], replicated
- moe_gain: bfloat16 [2048], replicated
- w_q: bfloat16 [2048, 3072], replicated
- w_dkv: bfloat16 [2048, 576], replicated
- w_uk: bfloat16 [16, 128, 512], replicated
- w_uv: bfloat16 [16, 512, 128], replicated
- w_o: bfloat16 [2048, 2048], replicated
- w_router: bfloat16 [2048, 64], replicated
- shared_gate: bfloat16 [2048, 2816], replicated
- shared_up: bfloat16 [2048, 2816], replicated
- shared_down: bfloat16 [2816, 2048], replicated
- expert_gate: bfloat16 [64, 2048, 1408], P('dp')
- expert_up: bfloat16 [64, 2048, 1408], P('dp')
- expert_down: bfloat16 [64, 1408, 2048], P('dp')
Outputs:
- output 1: bfloat16 [1024, 2048], P(('rep', 'dp')), parts along dimension 0
- output 2: bfloat16 [1024, 512], P(('rep', 'dp')), parts along dimension 0
- output 3: bfloat16 [1024, 64], P(('rep', 'dp')), parts along dimension 0
There are 2 independent parts. A program takes and returns all parts, laid end to end along the dimension named above; an argument that names none is the same for every part.
All inputs are finite; a program needn't handle non-finite values.
Results may differ from a plain program's by a relative error of at most 0.0127322.
Values are sent between devices in bfloat16 or wider.
A program may use at most 768 MiB of HBM per device.

v0:
```python
import functools

import jax
import jax.numpy as jnp
from jax import lax
from jax.experimental import pallas as pl
from jax.experimental.pallas import tpu as pltpu
from jax.sharding import PartitionSpec as P

NORM_EPS = 1e-6
ROPE_THETA = 10000.0


def rms_norm(values, gain_vec):
    vals_f32 = values.astype(jnp.float32)
    inv_rms = lax.rsqrt(jnp.mean(vals_f32 * vals_f32, axis=-1, keepdims=True) + NORM_EPS)
    return (vals_f32 * inv_rms * gain_vec.astype(jnp.float32)).astype(jnp.bfloat16)


def rope_tables(positions, rope_dim):
    inv_freq = ROPE_THETA ** (-2.0 * jnp.arange(rope_dim // 2, dtype=jnp.float32) / rope_dim)
    angles = positions.astype(jnp.float32)[:, None] * inv_freq[None, :]
    return jnp.cos(angles), jnp.sin(angles)


def apply_rope(values, rope_cos, rope_sin):
    half_dim = values.shape[-1] // 2
    first_half = values[..., :half_dim]
    second_half = values[..., half_dim:]
    return jnp.concatenate([first_half * rope_cos - second_half * rope_sin, second_half * rope_cos + first_half * rope_sin], axis=-1)


def attention_block(hidden, ckv_cache, kr_cache, seq_lens, attn_gain, kv_gain, w_q, w_dkv, w_uk, w_uv, w_o):
    batch_rows = hidden.shape[0]
    num_heads, nope_dim, value_a8 = w_uk.shape
    rope_dim = kr_cache.shape[-1]
    cache_len = ckv_cache.shape[1]
    score_scale = (nope_dim + rope_dim) ** -0.5
    normed_x = rms_norm(hidden, attn_gain)
    q_all = jnp.dot(normed_x, w_q, preferred_element_type=jnp.float32).astype(jnp.bfloat16).reshape(batch_rows, num_heads, nope_dim + rope_dim)
    latent_kv = jnp.dot(normed_x, w_dkv, preferred_element_type=jnp.float32)
    ckv_new = rms_norm(latent_kv[:, :value_a8], kv_gain)
    rope_cos, rope_sin = rope_tables(seq_lens, rope_dim)
    kr_new = apply_rope(latent_kv[:, value_a8:], rope_cos, rope_sin).astype(jnp.bfloat16)
    q_rot = apply_rope(q_all[:, :, nope_dim:].astype(jnp.float32), rope_cos[:, None, :], rope_sin[:, None, :]).astype(jnp.bfloat16)
    q_lat = jnp.einsum('bhn,hnc->bhc', q_all[:, :, :nope_dim], w_uk, preferred_element_type=jnp.float32).astype(jnp.bfloat16)
    scores = (jnp.einsum('bhc,blc->bhl', q_lat, ckv_cache, preferred_element_type=jnp.float32) + jnp.einsum('bhr,blr->bhl', q_rot, kr_cache, preferred_element_type=jnp.float32)) * score_scale
    valid_mask = jnp.arange(cache_len)[None, None, :] < seq_lens[:, None, None]
    scores = jnp.where(valid_mask, scores, -jnp.inf)
    new_score = (jnp.einsum('bhc,bc->bh', q_lat, ckv_new, preferred_element_type=jnp.float32) + jnp.einsum('bhr,br->bh', q_rot, kr_new, preferred_element_type=jnp.float32)) * score_scale
    top_score = jnp.maximum(jnp.max(scores, axis=-1), new_score)
    exp_cache = jnp.exp(scores - top_score[:, :, None])
    exp_new = jnp.exp(new_score - top_score)
    denominator = jnp.sum(exp_cache, axis=-1) + exp_new
    prob_cache = (exp_cache / denominator[:, :, None]).astype(jnp.bfloat16)
    prob_new = (exp_new / denominator).astype(jnp.bfloat16)
    o_lat = (jnp.einsum('bhl,blc->bhc', prob_cache, ckv_cache, preferred_element_type=jnp.float32) + jnp.einsum('bh,bc->bhc', prob_new, ckv_new, preferred_element_type=jnp.float32)).astype(jnp.bfloat16)
    head_out = jnp.einsum('bhc,hcv->bhv', o_lat, w_uv, preferred_element_type=jnp.float32).astype(jnp.bfloat16).reshape(batch_rows, -1)
    resid_out = (hidden.astype(jnp.float32) + jnp.dot(head_out, w_o, preferred_element_type=jnp.float32)).astype(jnp.bfloat16)
    return resid_out, ckv_new, kr_new


MESH_ID = pl.DeviceIdType.MESH


def silu(value):
    return value * (1.0 / (1.0 + jnp.exp(-value)))


def moe_kernel(dims, resid_ref, ids_ref, gain_ref, router_ref, sgate_hbm, sup_hbm, sdown_hbm, egate_hbm, eup_hbm, edown_hbm, out_ref,
               ublk, tokx, midx, send, recv, acc, table, tail, gu_buf, dn_buf,
               gu_sem, dn_sem, us_sem, ur_sem, ys_sem, yr_sem):
    group, experts_dev, experts, cap, depth, rep_axis, dp_axis = dims
    rows, width = resid_ref.shape
    half = rows // 2
    ff = gu_buf.shape[-1]
    n_shared = sgate_hbm.shape[-1] // ff
    steps = experts_dev + n_shared
    slot16 = 16
    slots = group * slot16
    main = send.shape[-1]
    blk = main // 3
    top_k = ids_ref.shape[-1]
    lanes = 128
    me = lax.axis_index(dp_axis)
    chips = group // 2
    core = lax.rem(me, 2)
    chip = me // 2
    partner = chip * 2 + (1 - core)
    left = lax.rem(chip + chips - 1, chips) * 2 + core
    right = lax.rem(chip + 1, chips) * 2 + core
    far = lax.rem(chip + 2, chips) * 2 + core

    def weights_gu(step, which, hbm, shared_hbm, action):
        slot = lax.rem(step, depth)

        @pl.when(step < experts_dev)
        def _():
            getattr(pltpu.make_async_copy(hbm.at[step], gu_buf.at[slot, which], gu_sem.at[slot, which]), action)()

        @pl.when(step >= experts_dev)
        def _():
            cols = pl.ds(pl.multiple_of((step - experts_dev) * ff, 128), ff)
            getattr(pltpu.make_async_copy(shared_hbm.at[:, cols], gu_buf.at[slot, which], gu_sem.at[slot, which]), action)()

    def weights_dn(step, action):
        slot = lax.rem(step, depth)

        @pl.when(step < experts_dev)
        def _():
            getattr(pltpu.make_async_copy(edown_hbm.at[step], dn_buf.at[slot], dn_sem.at[slot]), action)()

        @pl.when(step >= experts_dev)
        def _():
            cols = pl.ds(pl.multiple_of((step - experts_dev) * ff, 128), ff)
            getattr(pltpu.make_async_copy(sdown_hbm.at[cols], dn_buf.at[slot], dn_sem.at[slot]), action)()

    def fetch(step):
        weights_gu(step, 0, egate_hbm, sgate_hbm, "start")
        weights_gu(step, 1, eup_hbm, sup_hbm, "start")

    for first in range(depth):
        fetch(jnp.int32(first))
        weights_dn(jnp.int32(first), "start")

    barrier = pltpu.get_barrier_semaphore()
    for k in range(1, group):
        pl.semaphore_signal(barrier, inc=1, device_id={dp_axis: lax.rem(me + k, group)}, device_id_type=MESH_ID)

    resid = resid_ref[...].astype(jnp.float32)
    inv = lax.rsqrt(jnp.mean(resid * resid, axis=-1, keepdims=True) + NORM_EPS)
    u = (resid * inv * gain_ref[...].astype(jnp.float32)).astype(jnp.bfloat16)
    lane = lax.broadcasted_iota(jnp.int32, (rows, lanes), 1)
    picked = jnp.zeros((rows, lanes), jnp.bool_)
    for k in range(top_k):
        picked = picked | (ids_ref[:, k:k + 1] == lane)
    lower = (lax.broadcasted_iota(jnp.int32, (rows, rows), 1) < lax.broadcasted_iota(jnp.int32, (rows, rows), 0)).astype(jnp.float32).astype(jnp.bfloat16)
    rank = jnp.dot(lower, jnp.where(picked, 1.0, 0.0).astype(jnp.bfloat16), preferred_element_type=jnp.float32)
    codes = jnp.where(picked, rank, -1.0).astype(jnp.bfloat16)
    for h in range(2):
        ublk[me, h, :, :width] = u[h * half:(h + 1) * half]
        ublk[me, h, :, width:] = codes[h * half:(h + 1) * half]
    logits = jnp.dot(u, router_ref[...], preferred_element_type=jnp.float32)
    logits = logits - jnp.max(logits, axis=-1, keepdims=True)
    expl = jnp.exp(logits)
    prob = expl / jnp.sum(expl, axis=-1, keepdims=True)
    prob = jnp.concatenate([prob, jnp.zeros((rows, lanes - experts), jnp.float32)], axis=-1)
    p0 = prob.astype(jnp.bfloat16)
    rest = prob - p0.astype(jnp.float32)
    p1 = rest.astype(jnp.bfloat16)
    p2 = (rest - p1.astype(jnp.float32)).astype(jnp.bfloat16)
    table[0] = codes
    table[1] = p0
    table[2] = p1
    table[3] = p2
    acc[...] = resid

    pl.semaphore_wait(barrier, group - 1)

    def block_copy(block, h, dest, sem_no):
        return pltpu.make_async_remote_copy(src_ref=ublk.at[block, h], dst_ref=ublk.at[block, h], send_sem=us_sem.at[sem_no], recv_sem=ur_sem.at[block, h], device_id={dp_axis: dest}, device_id_type=MESH_ID)

    copies = []

    def send_block(block, h, dest):
        copy = block_copy(block, h, dest, len(copies))
        copy.start()
        copies.append(copy)

    def arrived(block, h):
        block_copy(block, h, partner, 0).wait_recv()

    send_block(me, 0, right)
    send_block(me, 1, left)
    send_block(me, 1, right)
    send_block(me, 0, left)
    send_block(me, 0, partner)
    send_block(me, 1, partner)
    arrived(left, 0)
    send_block(left, 0, right)
    send_block(left, 0, partner)
    arrived(right, 1)
    send_block(right, 1, left)
    send_block(right, 1, partner)
    arrived(left, 1)
    send_block(left, 1, partner)
    arrived(right, 0)
    send_block(right, 0, partner)
    arrived(far, 0)
    send_block(far, 0, partner)
    arrived(far, 1)
    send_block(far, 1, partner)
    for block in (partner, lax.rem(left + 1 - 2 * core + group, group), lax.rem(right + 1 - 2 * core + group, group), lax.rem(far + 1 - 2 * core + group, group)):
        for h in range(2):
            arrived(block, h)

    row_i = lax.broadcasted_iota(jnp.int32, (lanes, slots), 0)
    col_i = lax.broadcasted_iota(jnp.int32, (lanes, slots), 1)

    def return_copy(step, dest):
        return pltpu.make_async_remote_copy(src_ref=send.at[step, dest], dst_ref=recv.at[step, me], send_sem=ys_sem.at[step, dest], recv_sem=yr_sem.at[step, me], device_id={dp_axis: dest}, device_id_type=MESH_ID)

    def arrival(step, source):
        return pltpu.make_async_remote_copy(src_ref=send.at[step, source], dst_ref=recv.at[step, source], send_sem=ys_sem.at[step, source], recv_sem=yr_sem.at[step, source], device_id={dp_axis: source}, device_id_type=MESH_ID)

    def gather_rows(step):
        pick = (row_i == me * experts_dev + step).astype(jnp.float32).astype(jnp.bfloat16)
        code_all = ublk[:, :, :, width:].reshape(group * rows, lanes)
        code_b = jnp.dot(code_all, pick, preferred_element_type=jnp.float32)
        tok = lax.broadcasted_iota(jnp.int32, (group * rows, slots), 0)
        col = lax.broadcasted_iota(jnp.int32, (group * rows, slots), 1)
        hit = (code_b == lax.rem(col, slot16).astype(jnp.float32)) & (tok // rows == col // slot16)
        place = jnp.where(hit, 1.0, 0.0).astype(jnp.bfloat16)
        for c0 in range(0, width, 512):
            rows_u = ublk[:, :, :, c0:c0 + 512].reshape(group * rows, 512)
            picked_rows = lax.dot_general(place, rows_u, (((0,), (0,)), ((), ())), preferred_element_type=jnp.float32)
            tokx[:, c0:c0 + 512] = picked_rows.astype(jnp.bfloat16)

    def pack_block(y_main, q):
        y_main = y_main.reshape(group, 2, 8, blk)
        y_tail = tail[...].reshape(group, 2, 8, blk)
        sub = lax.broadcasted_iota(jnp.int32, (group, 8, blk), 1)
        part = y_tail[:, 1 if q == 2 else 0]
        if q != 1:
            part = pltpu.roll(part.reshape(group * 8, blk).reshape(group, 8, blk), 4, 1)
        low = jnp.where(sub >= 4, part, y_main[:, 1])
        return jnp.concatenate([y_main[:, 0], low], axis=1).astype(jnp.bfloat16)

    def combine(step):
        for k in range(1, group):
            arrival(step, lax.rem(me + k, group)).wait_recv()
        spread = (row_i == (col_i // slot16) * experts_dev + step).astype(jnp.float32).astype(jnp.bfloat16)
        wide = jnp.dot(table[...].reshape(4 * rows, lanes), spread, preferred_element_type=jnp.float32)
        code_b = wide[:rows]
        slot_i = lax.rem(lax.broadcasted_iota(jnp.int32, (rows, slots), 1), slot16)
        slot_f = slot_i.astype(jnp.float32)
        for q in range(3):
            hits = [code_b == slot_f, (slot_i >= cap) & (code_b == slot_f - cap + 4 * q)]
            lhs = jnp.concatenate([jnp.where(hit, wide[p * rows:(p + 1) * rows], 0.0) for hit in hits for p in (1, 2, 3)], axis=0).astype(jnp.bfloat16)
            y_blk = recv[step, :, :, q * blk:(q + 1) * blk].reshape(slots, blk)
            res = jnp.dot(lhs, y_blk, preferred_element_type=jnp.float32)
            acc[:, q * blk:(q + 1) * blk] += res[:rows] + (res[rows:2 * rows] + res[2 * rows:3 * rows])
            acc[:, main:] += res[3 * rows:4 * rows] + (res[4 * rows:5 * rows] + res[5 * rows:])

    def one_step(step, carry):
        slot = lax.rem(step, depth)
        is_routed = step < experts_dev

        @pl.when(is_routed)
        def _():
            gather_rows(step)

        @pl.when(step == experts_dev)
        def _():
            tokx[:rows] = ublk[me, :, :, :width].reshape(rows, width)
            tokx[rows:] = jnp.zeros((slots - rows, width), jnp.bfloat16)

        weights_gu(step, 0, egate_hbm, sgate_hbm, "wait")
        weights_gu(step, 1, eup_hbm, sup_hbm, "wait")
        for c0 in range(0, ff, 512):
            c1 = min(c0 + 512, ff)
            gate_act = jnp.dot(tokx[...], gu_buf[slot, 0, :, c0:c1], preferred_element_type=jnp.float32)
            up_act = jnp.dot(tokx[...], gu_buf[slot, 1, :, c0:c1], preferred_element_type=jnp.float32)
            midx[:, c0:c1] = (silu(gate_act) * up_act).astype(jnp.bfloat16)

        @pl.when(step + depth < steps)
        def _():
            fetch(step + depth)

        weights_dn(step, "wait")
        tail[...] = jnp.dot(midx[...], dn_buf[slot, :, main:], preferred_element_type=jnp.float32)

        @pl.when(step >= experts_dev)
        def _():
            acc[:, main:] += tail[:rows]

        for q in range(3):
            y_main = jnp.dot(midx[...], dn_buf[slot, :, q * blk:(q + 1) * blk], preferred_element_type=jnp.float32)

            @pl.when(is_routed)
            def _():
                send[step, :, :, q * blk:(q + 1) * blk] = pack_block(y_main, q)

            @pl.when(step >= experts_dev)
            def _():
                acc[:, q * blk:(q + 1) * blk] += y_main[:rows]

        @pl.when(step + depth < steps)
        def _():
            weights_dn(step + depth, "start")

        @pl.when(is_routed)
        def _():
            recv[step, me] = send[step, me]
            for k in (4, 3, 5, 2, 6, 1, 7):
                return_copy(step, lax.rem(me + k, group)).start()

        @pl.when(step >= steps - experts_dev)
        def _():
            combine(step - (steps - experts_dev))

        return carry

    lax.fori_loop(0, steps, one_step, 0)
    out_ref[...] = acc[...].astype(out_ref.dtype)

    for copy in copies:
        copy.wait_send()

    def drain(step, carry):
        for k in range(1, group):
            return_copy(step, lax.rem(me + k, group)).wait_send()
        return carry

    lax.fori_loop(0, experts_dev, drain, 0)


def moe_layer(resid_out, expert_ids, cap, group, moe_gain, w_router, shared_gate, shared_up, shared_down, expert_gate, expert_up, expert_down):
    rows, width = resid_out.shape
    experts_dev, _, ff = expert_gate.shape
    experts = w_router.shape[1]
    depth = 3
    main = 3 * width // 4
    slots = group * 16
    dims = (group, experts_dev, experts, cap, depth, 'rep', 'dp')
    vmem = pl.BlockSpec(memory_space=pltpu.VMEM)
    hbm = pl.BlockSpec(memory_space=pl.ANY)
    return pl.pallas_call(
        functools.partial(moe_kernel, dims),
        out_shape=jax.ShapeDtypeStruct((rows, width), jnp.bfloat16),
        in_specs=[vmem] * 4 + [hbm] * 6,
        out_specs=vmem,
        scratch_shapes=[
            pltpu.VMEM((group, 2, rows // 2, width + 128), jnp.bfloat16),
            pltpu.VMEM((slots, width), jnp.bfloat16),
            pltpu.VMEM((slots, ff), jnp.bfloat16),
            pltpu.VMEM((experts_dev, group, 16, main), jnp.bfloat16),
            pltpu.VMEM((experts_dev, group, 16, main), jnp.bfloat16),
            pltpu.VMEM((rows, width), jnp.float32),
            pltpu.VMEM((4, rows, 128), jnp.bfloat16),
            pltpu.VMEM((slots, width - main), jnp.float32),
            pltpu.VMEM((depth, 2, width, ff), jnp.bfloat16),
            pltpu.VMEM((depth, ff, width), jnp.bfloat16),
            pltpu.SemaphoreType.DMA((depth, 2)),
            pltpu.SemaphoreType.DMA((depth,)),
            pltpu.SemaphoreType.DMA((14,)),
            pltpu.SemaphoreType.DMA((group, 2)),
            pltpu.SemaphoreType.DMA((experts_dev, group)),
            pltpu.SemaphoreType.DMA((experts_dev, group)),
        ],
        compiler_params=pltpu.CompilerParams(collective_id=0, has_side_effects=True, vmem_limit_bytes=67043328),
        name='moe_layer',
    )(resid_out, expert_ids, moe_gain.reshape(1, -1), w_router, shared_gate, shared_up, shared_down, expert_gate, expert_up, expert_down)


def solution(mesh):
    row_spec = P(('rep', 'dp'))
    full_spec = P()
    expert_spec = P('dp')

    def device_step(hidden, ckv_cache, kr_cache, seq_lens, expert_ids, attn_gain, kv_gain, moe_gain, w_q, w_dkv, w_uk, w_uv, w_o, w_router, shared_gate, shared_up, shared_down, expert_gate, expert_up, expert_down):
        capacity = max(2, 2 * hidden.shape[0] * expert_ids.shape[1] // w_router.shape[1])
        resid_out, ckv_new, kr_new = attention_block(hidden, ckv_cache, kr_cache, seq_lens, attn_gain, kv_gain, w_q, w_dkv, w_uk, w_uv, w_o)
        layer_out = moe_layer(resid_out, expert_ids, capacity, mesh.shape['dp'], moe_gain, w_router, shared_gate, shared_up, shared_down, expert_gate, expert_up, expert_down)
        return layer_out, ckv_new, kr_new

    in_specs = (row_spec,) * 5 + (full_spec,) * 12 + (expert_spec,) * 3
    return jax.shard_map(device_step, mesh=mesh, in_specs=in_specs, out_specs=(row_spec, row_spec, row_spec), check_vma=False)
```

profile of v0, /device:TPU:113, one launch (start us, length us, event | category | flops | bytes accessed | tf_op | source)
XLA Modules:
  0.0 115.9 jit_solution(1779539655038730982)
XLA Ops:
  0.7 0.7 convert_element_type.52
  1.4 1.1 fusion.14
  2.5 2.6 %fusion.24 = f32[64,576]{1,0:T(8,128)S(1)} fusion(bf16[2048,576]{0,1:T(8,128)(2,1)} %param.29, bf16[64,2048]{1,0:T(8,128)(2,1)} %param.20, f32[2048]{0:T(1024)S(1)} %convert_element_type.52, f32[64]{0:T(128)S(1)} %add_rsqrt_fusion.1), kind=kOutput, calls=%fused_computation.39 | convolution fusion | flops 151519232 | bytes 2777344 | tf_op jit(solution)/shard_map/dot_general | solution.py:41
  5.1 0.2 subtract_convert_fusion.1
  5.4 6.9 %convolution_convert_fusion = bf16[64,3072]{1,0:T(8,128)(2,1)S(1)} fusion(bf16[2048,3072]{1,0:T(8,128)(2,1)} %param.28, bf16[64,2048]{1,0:T(8,128)(2,1)S(1)} %copy-done, f32[2048]{0:T(1024)S(1)} %convert_element_type.52, f32[64]{0:T(128)S(1)} %add_rsqrt_fusion.1), kind=kOutput, calls=%fused_computation | convolution fusion | flops 806027264 | bytes 13246720 | tf_op jit(solution)/shard_map/dot_general | solution.py:40
  12.3 0.6 reshape.106
  13.0 0.2 subtract_convert_fusion
  13.3 0.3 fusion.27
  13.7 0.8 copy-done.1
  14.5 0.4 fusion.2
  15.0 10.2 %fusion.12 = f32[64,16,256]{2,1,0:T(8,128)S(1)} fusion(bf16[64,256,512]{2,1,0:T(8,128)(2,1)} %param.21, bf16[64,16,512]{2,0,1:T(8,128)(2,1)S(1)} %fusion.2), kind=kOutput, calls=%fused_computation.19 | convolution fusion | flops 268435456 | bytes 18874368 | tf_op jit(solution)/shard_map/bhc,blc->bhl/dot_general | solution.py:47
  25.3 2.2 %fusion.35 = (f32[64,16]{1,0:T(8,128)S(1)}, f32[64,16,256]{2,1,0:T(8,128)S(1)}) fusion(f32[64,16,256]{2,1,0:T(8,128)S(1)} %fusion.12, bf16[64,256,64]{1,2,0:T(8,128)(2,1)} %param.22, bf16[64,16,32]{2,1,0:T(8,128)(2,1)S(1)} %get-tuple-element.6, bf16[64,16,32]{2,1,0:T(8,128)(2,1)S(1)} %get-tuple-element.5, pred[64,256]{1,0:T(8,128)(4,1)S(1)} %iota_compare_fusion), kind=kOutput, calls=%fused_computation.60 | convolution fusion | flops 34864128 | bytes 4345856 | tf_op jit(solution)/shard_map/bhr,blr->bhl/dot_general | solution.py:47
  27.5 0.1 multiply_reduce_fusion
  27.8 0.7 fusion.10
  28.5 0.4 fusion.9
  28.9 7.2 %fusion.17 = f32[64,16,512]{2,1,0:T(8,128)S(1)} fusion(bf16[64,256,512]{2,1,0:T(8,128)(2,1)} %param.21, f32[64,16,256]{2,1,0:T(8,128)S(1)} %get-tuple-element.14, f32[64,16]{1,0:T(8,128)S(1)} %get-tuple-element.10, f32[64,16]{1,0:T(8,128)S(1)} %fusion.30), kind=kOutput, calls=%fused_computation.26 | convolution fusion | flops 269221888 | bytes 19931136 | tf_op jit(solution)/shard_map/bhl,blc->bhc/dot_general | solution.py:57
  36.2 3.0 %fusion.5 = bf16[16,8,8,128]{3,2,1,0:T(8,128)(2,1)S(1)} fusion(bf16[16,512,128]{2,1,0:T(8,128)(2,1)} %param.31, f32[64,16,512]{2,1,0:T(8,128)S(1)} %fusion.17, f32[64,512]{1,0:T(8,128)S(1)} %get-tuple-element.3, f32[64,16]{0,1:T(8,128)S(1)} %copy.30), kind=kOutput, calls=%fused_computation.11 | convolution fusion | flops 135921664 | bytes 4591616 | tf_op jit(solution)/shard_map/bhc,hcv->bhv/dot_general | solution.py:58
  39.2 5.7 %fusion.resid_ref = bf16[64,2048]{1,0:T(8,128)(2,1)} fusion(bf16[2048,2048]{1,0:T(8,128)(2,1)} %param.32, bf16[64,2048]{1,0:T(8,128)(2,1)S(1)} %copy-done, bf16[16,8,8,128]{3,2,1,0:T(8,128)(2,1)S(1)} %fusion.5), kind=kOutput, calls=%fused_computation.2 | convolution fusion | flops 537264128 | bytes 9175040 | tf_op jit(solution)/shard_map/dot_general | solution.py:59
  45.0 1.0 copy.33.router_ref
  46.0 0.7 copy.32.ids_ref
  46.7 0.6 reshape.108.gain_ref
  47.3 65.6 %moe_layer.1 = bf16[64,2048]{1,0:T(8,128)(2,1)} custom-call(bf16[64,2048]{1,0:T(8,128)(2,1)} %fusion.resid_ref, s32[64,6]{1,0:T(8,128)} %copy.32.ids_ref, bf16[1,2048]{1,0:T(2,128)(2,1)} %reshape.108.gain_ref, bf16[2048,64]{1,0:T(8,128)(2,1)} %copy.33.router_ref, bf16[2048,2816]{1,0:T(8,128)(2,1)} %sgate_hbm.1, bf16[2048,2816]{1,0:T(8,128)(2,1)} %sup_hbm.1, ...), custom_call_target="tpu_custom_call" | custom-call | tf_op jit(solution)/shard_map/moe_layer/pallas_call | solution.py:328
  112.9 1.4 %pad_maximum_fusion.3 = bf16[64,64]{1,0:T(8,128)(2,1)} fusion(bf16[64,32]{1,0:T(8,128)(2,1)} %copy-done.4, bf16[64,32]{1,0:T(8,128)(2,1)} %copy-done.3), kind=kLoop, calls=%fused_computation.51 | loop fusion | flops 16384 | bytes 16384 | tf_op jit(solution)/shard_map/concatenate | solution.py:30
  114.3 1.7 %copy.60 = bf16[64,2048]{1,0:T(8,128)(2,1)} copy(bf16[64,2048]{1,0:T(8,128)(2,1)} %moe_layer.1) | data formatting | bytes 524288
  (32 shorter events, 0.5 us)
Async XLA Ops:
  0.6 4.7 %copy-start = (bf16[64,2048]{1,0:T(8,128)(2,1)S(1)}, bf16[64,2048]{1,0:T(8,128)(2,1)}, u32[]{:S(2)}) copy-start(bf16[64,2048]{1,0:T(8,128)(2,1)} %param.20) | copy-start | bytes 786436
  0.6 4.5 %copy-start.9 = (s32[64]{0:T(128)S(1)}, s32[64]{0:T(128)}, u32[]{:S(2)}) copy-start(s32[64]{0:T(128)} %param.23) | copy-start | bytes 772
  5.3 7.9 %copy-start.3 = (bf16[64,32]{1,0:T(8,128)(2,1)}, bf16[64,32]{1,0:T(8,128)(2,1)S(1)}, u32[]{:S(2)}) copy-start(bf16[64,32]{1,0:T(8,128)(2,1)S(1)} %get-tuple-element.7) | copy-start | bytes 12292
  5.4 7.9 %copy-start.4 = (bf16[64,32]{1,0:T(8,128)(2,1)}, bf16[64,32]{1,0:T(8,128)(2,1)S(1)}, u32[]{:S(2)}) copy-start(bf16[64,32]{1,0:T(8,128)(2,1)S(1)} %get-tuple-element.8) | copy-start | bytes 12292
  12.9 1.6 %copy-start.1 = (bf16[16,128,512]{2,1,0:T(8,128)(2,1)S(1)}, bf16[16,128,512]{2,1,0:T(8,128)(2,1)}, u32[]{:S(2)}) copy-start(bf16[16,128,512]{2,1,0:T(8,128)(2,1)} %param.30) | copy-start | bytes 6291460
  25.3 2.3 %copy-start.8 = (bf16[512]{0:T(512)(128)(2,1)S(1)}, bf16[512]{0:T(512)(128)(2,1)}, u32[]{:S(2)}) copy-start(bf16[512]{0:T(512)(128)(2,1)} %param.26) | copy-start | bytes 3076
  27.7 8.3 %copy-start.5 = (bf16[64,512]{1,0:T(8,128)(2,1)}, bf16[64,512]{1,0:T(8,128)(2,1)S(1)}, u32[]{:S(2)}) copy-start(bf16[64,512]{1,0:T(8,128)(2,1)S(1)} %get-tuple-element.19) | copy-start | bytes 196612
  39.2 5.8 %copy-start.2 = (bf16[2048,64]{0,1:T(8,128)(2,1)S(1)}, bf16[2048,64]{0,1:T(8,128)(2,1)}, u32[]{:S(2)}) copy-start(bf16[2048,64]{0,1:T(8,128)(2,1)} %param.33) | copy-start | bytes 786436
  39.2 6.8 %copy-start.6 = (s32[64,6]{0,1:T(8,128)S(1)}, s32[64,6]{0,1:T(8,128)}, u32[]{:S(2)}) copy-start(s32[64,6]{0,1:T(8,128)} %param.24) | copy-start | bytes 4612
  39.2 7.5 %copy-start.7 = (bf16[2048]{0:T(1024)(128)(2,1)S(1)}, bf16[2048]{0:T(1024)(128)(2,1)}, u32[]{:S(2)}) copy-start(bf16[2048]{0:T(1024)(128)(2,1)} %param.27) | copy-start | bytes 12292
where the time goes:
time: 116 us
  Pallas kernels  65.6 us (57%)
  matrix products  39.4 us (34%)
  local copies, waits for them, and re-layouts  5.55 us (5%)
  other arithmetic  4.54 us (4%)
    pallas_call x1, Pallas kernels, moe_layer(): pl.pallas_call(functools.partial(moe_kernel, dims), out_shape=jax.ShapeDt...  65.6 us
    dot_general x1, matrix products, attention_block(): jnp.einsum('bhc,blc->bhl', q_lat, ckv_cache, preferred_element_type=jnp.f...  10.2 us
    dot_general x1, matrix products, attention_block(): jnp.einsum('bhl,blc->bhc', prob_cache, ckv_cache, preferred_element_type=...  7.21 us
    dot_general x1, matrix products, attention_block(): jnp.dot(normed_x, w_q, preferred_element_type=jnp.float32)  6.95 us
    dot_general x1, matrix products, attention_block(): jnp.dot(head_out, w_o, preferred_element_type=jnp.float32)  5.74 us
    unnamed x23, local copies, waits for them, and re-layouts  4.22 us
    dot_general x1, matrix products, attention_block(): jnp.einsum('bhc,hcv->bhv', o_lat, w_uv, preferred_element_type=jnp.float32)  3.01 us
    dot_general x1, matrix products, attention_block(): latent_kv = jnp.dot(normed_x, w_dkv, preferred_element_type=jnp.float32)  2.59 us

commit v1 on v0

--- a/solution.py
+++ b/solution.py
@@ -1,4 +1,5 @@
 import functools
+import math
 
 import jax
 import jax.numpy as jnp
@@ -9,55 +10,6 @@
 
 NORM_EPS = 1e-6
 ROPE_THETA = 10000.0
-
-
-def rms_norm(values, gain_vec):
-    vals_f32 = values.astype(jnp.float32)
-    inv_rms = lax.rsqrt(jnp.mean(vals_f32 * vals_f32, axis=-1, keepdims=True) + NORM_EPS)
-    return (vals_f32 * inv_rms * gain_vec.astype(jnp.float32)).astype(jnp.bfloat16)
-
-
-def rope_tables(positions, rope_dim):
-    inv_freq = ROPE_THETA ** (-2.0 * jnp.arange(rope_dim // 2, dtype=jnp.float32) / rope_dim)
-    angles = positions.astype(jnp.float32)[:, None] * inv_freq[None, :]
-    return jnp.cos(angles), jnp.sin(angles)
-
-
-def apply_rope(values, rope_cos, rope_sin):
-    half_dim = values.shape[-1] // 2
-    first_half = values[..., :half_dim]
-    second_half = values[..., half_dim:]
-    return jnp.concatenate([first_half * rope_cos - second_half * rope_sin, second_half * rope_cos + first_half * rope_sin], axis=-1)
-
-
-def attention_block(hidden, ckv_cache, kr_cache, seq_lens, attn_gain, kv_gain, w_q, w_dkv, w_uk, w_uv, w_o):
-    batch_rows = hidden.shape[0]
-    num_heads, nope_dim, value_a8 = w_uk.shape
-    rope_dim = kr_cache.shape[-1]
-    cache_len = ckv_cache.shape[1]
-    score_scale = (nope_dim + rope_dim) ** -0.5
-    normed_x = rms_norm(hidden, attn_gain)
-    q_all = jnp.dot(normed_x, w_q, preferred_element_type=jnp.float32).astype(jnp.bfloat16).reshape(batch_rows, num_heads, nope_dim + rope_dim)
-    latent_kv = jnp.dot(normed_x, w_dkv, preferred_element_type=jnp.float32)
-    ckv_new = rms_norm(latent_kv[:, :value_a8], kv_gain)
-    rope_cos, rope_sin = rope_tables(seq_lens, rope_dim)
-    kr_new = apply_rope(latent_kv[:, value_a8:], rope_cos, rope_sin).astype(jnp.bfloat16)
-    q_rot = apply_rope(q_all[:, :, nope_dim:].astype(jnp.float32), rope_cos[:, None, :], rope_sin[:, None, :]).astype(jnp.bfloat16)
-    q_lat = jnp.einsum('bhn,hnc->bhc', q_all[:, :, :nope_dim], w_uk, preferred_element_type=jnp.float32).astype(jnp.bfloat16)
-    scores = (jnp.einsum('bhc,blc->bhl', q_lat, ckv_cache, preferred_element_type=jnp.float32) + jnp.einsum('bhr,blr->bhl', q_rot, kr_cache, preferred_element_type=jnp.float32)) * score_scale
-    valid_mask = jnp.arange(cache_len)[None, None, :] < seq_lens[:, None, None]
-    scores = jnp.where(valid_mask, scores, -jnp.inf)
-    new_score = (jnp.einsum('bhc,bc->bh', q_lat, ckv_new, preferred_element_type=jnp.float32) + jnp.einsum('bhr,br->bh', q_rot, kr_new, preferred_element_type=jnp.float32)) * score_scale
-    top_score = jnp.maximum(jnp.max(scores, axis=-1), new_score)
-    exp_cache = jnp.exp(scores - top_score[:, :, None])
-    exp_new = jnp.exp(new_score - top_score)
-    denominator = jnp.sum(exp_cache, axis=-1) + exp_new
-    prob_cache = (exp_cache / denominator[:, :, None]).astype(jnp.bfloat16)
-    prob_new = (exp_new / denominator).astype(jnp.bfloat16)
-    o_lat = (jnp.einsum('bhl,blc->bhc', prob_cache, ckv_cache, preferred_element_type=jnp.float32) + jnp.einsum('bh,bc->bhc', prob_new, ckv_new, preferred_element_type=jnp.float32)).astype(jnp.bfloat16)
-    head_out = jnp.einsum('bhc,hcv->bhv', o_lat, w_uv, preferred_element_type=jnp.float32).astype(jnp.bfloat16).reshape(batch_rows, -1)
-    resid_out = (hidden.astype(jnp.float32) + jnp.dot(head_out, w_o, preferred_element_type=jnp.float32)).astype(jnp.bfloat16)
-    return resid_out, ckv_new, kr_new
 
 
 MESH_ID = pl.DeviceIdType.MESH
@@ -140,7 +92,7 @@
     for h in range(2):
         ublk[me, h, :, :width] = u[h * half:(h + 1) * half]
         ublk[me, h, :, width:] = codes[h * half:(h + 1) * half]
-    logits = jnp.dot(u, router_ref[...], preferred_element_type=jnp.float32)
+    logits = lax.dot_general(u, router_ref[...], (((1,), (1,)), ((), ())), preferred_element_type=jnp.float32)
     logits = logits - jnp.max(logits, axis=-1, keepdims=True)
     expl = jnp.exp(logits)
     prob = expl / jnp.sum(expl, axis=-1, keepdims=True)
@@ -350,7 +302,230 @@
         ],
         compiler_params=pltpu.CompilerParams(collective_id=0, has_side_effects=True, vmem_limit_bytes=67043328),
         name='moe_layer',
-    )(resid_out, expert_ids, moe_gain.reshape(1, -1), w_router, shared_gate, shared_up, shared_down, expert_gate, expert_up, expert_down)
+    )(resid_out, expert_ids, moe_gain.reshape(1, -1), w_router.T, shared_gate, shared_up, shared_down, expert_gate, expert_up, expert_down)
+
+
+def attention_phase(refs, hooks):
+    (hidden_ref, lens_ref, again_ref, kgain_ref, ckv_hbm, krt_hbm, wq_hbm, dkvt_hbm, uk_hbm, uv_hbm, wo_hbm, cnew_ref, knew_ref,
+     tokx, uvbuf, gu_buf, dn_buf, qlat, qrot, newc, newk, pos, a_sem, c_sem) = refs
+    rows, width = hidden_ref.shape
+    lora = qlat.shape[-1]
+    heads = qlat.shape[1]
+    rope_dim = krt_hbm.shape[0] // rows
+    length = krt_hbm.shape[1]
+    nope = uk_hbm.shape[0] // heads
+    head_dim = nope + rope_dim
+    qcols = wq_hbm.shape[1] // 4
+    four = 4 * length
+    value_dim = uv_hbm.shape[1]
+    scale = head_dim ** -0.5
+    lanes = 128
+    lat0 = dn_buf.shape[1] - four
+    lat1 = dkvt_hbm.shape[0] - lat0
+    cache_cols = slice(qcols, qcols + lora)
+    kr_cols = slice(width // 2, width // 2 + length)
+
+    def query_copy(i):
+        return pltpu.make_async_copy(wq_hbm.at[:, i * qcols:(i + 1) * qcols], gu_buf.at[i // 2, i % 2, :, 0:qcols], a_sem.at[i])
+
+    latent_copies = [
+        pltpu.make_async_copy(dkvt_hbm.at[0:lat0], dn_buf.at[1, four:four + lat0], a_sem.at[4]),
+        pltpu.make_async_copy(dkvt_hbm.at[lat0:lat0 + lat1], dn_buf.at[2, four:four + lat1], a_sem.at[5]),
+    ]
+    uk_copy = pltpu.make_async_copy(uk_hbm, gu_buf.at[0, 1, :, cache_cols], a_sem.at[6])
+    kr_copies = [pltpu.make_async_copy(krt_hbm.at[w * width:(w + 1) * width], gu_buf.at[2, w, :, kr_cols], a_sem.at[7 + w]) for w in range(2)]
+    out_copies = [pltpu.make_async_copy(wo_hbm.at[:, w * (width // 2):(w + 1) * (width // 2)], gu_buf.at[2, w, :, 0:width // 2], a_sem.at[9 + w]) for w in range(2)]
+    uv_copies = [pltpu.make_async_copy(uv_hbm.at[i * 2 * lora:(i + 1) * 2 * lora], uvbuf.at[:, i * value_dim:(i + 1) * value_dim], a_sem.at[11 + i]) for i in range(heads // 2)]
+    wide_seqs = 48
+
+    def cache_copy(n):
+        if n >= 12:
+            w, r = (n - 12) // 2, n % 2
+            return pltpu.make_async_copy(ckv_hbm.at[n * four:(n + 1) * four], gu_buf.at[1, w, r * four:(r + 1) * four, cache_cols], c_sem.at[n])
+        return pltpu.make_async_copy(ckv_hbm.at[n * four:(n + 1) * four], dn_buf.at[n // 4, 0:four, (n % 4) * lora:(n % 4 + 1) * lora], c_sem.at[n])
+
+    query_copy(0).start()
+    for copy in latent_copies:
+        copy.start()
+    uk_copy.start()
+    for i in range(1, 4):
+        query_copy(i).start()
+
+    lane = lax.broadcasted_iota(jnp.int32, (rows, lanes), 1)
+    hidden = hidden_ref[...].astype(jnp.float32)
+    inv = lax.rsqrt(jnp.mean(hidden * hidden, axis=-1, keepdims=True) + NORM_EPS)
+    tokx[0:rows] = (hidden * inv * again_ref[...].astype(jnp.float32)).astype(jnp.bfloat16)
+    for b in range(rows):
+        pos[b:b + 1, :] = jnp.full((1, lanes), lens_ref[b], jnp.int32).astype(jnp.float32)
+    quarter = lax.rem(lane, rope_dim // 2).astype(jnp.float32)
+    angle = pos[...] * jnp.exp(quarter * (-2.0 / rope_dim * math.log(ROPE_THETA)))
+    rope_cos = jnp.cos(angle)
+    low_half = lax.rem(lane, rope_dim) < rope_dim // 2
+    rope_sin = jnp.where(low_half, -jnp.sin(angle), jnp.sin(angle))
+
+    def rope(value):
+        swapped = jnp.where(low_half, pltpu.roll(value, lanes - rope_dim // 2, 1), pltpu.roll(value, rope_dim // 2, 1))
+        return value * rope_cos + swapped * rope_sin
+
+    first_half = lane < rope_dim
+    for i in range(4):
+        query_copy(i).wait()
+        q_cols = jnp.dot(tokx[0:rows], gu_buf[i // 2, i % 2, :, 0:qcols], preferred_element_type=jnp.float32)
+        q_cols = q_cols.astype(jnp.bfloat16).astype(jnp.float32)
+        if i == 0:
+            for n in range(12, 16):
+                cache_copy(n).start()
+            for copy in kr_copies:
+                copy.start()
+            uk_copy.wait()
+        if i == 1:
+            for n in range(4):
+                cache_copy(n).start()
+        for pair in range(qcols // (2 * head_dim)):
+            base = pair * 2 * head_dim
+            tile0, tile1, tile2 = (q_cols[:, base + k * lanes:base + (k + 1) * lanes] for k in range(3))
+            head = i * (qcols // head_dim) + 2 * pair
+            nopes = (tile0, pltpu.roll(jnp.where(first_half, tile2, tile1), lanes // 2, 1))
+            turned = rope(jnp.where(first_half, tile1, tile2))
+            for odd in range(2):
+                h = head + odd
+                qrot[:, h, :] = pltpu.roll(turned, lanes // 2, 1) if odd else turned
+                uk_head = gu_buf[0, 1, h * nope:(h + 1) * nope, cache_cols]
+                qlat[:, h, :] = jnp.dot(nopes[odd].astype(jnp.bfloat16), uk_head, preferred_element_type=jnp.float32)
+    for n in range(4, 12):
+        cache_copy(n).start()
+    for copy in uv_copies + out_copies:
+        copy.start()
+    hooks[0]()
+
+    for copy in latent_copies:
+        copy.wait()
+    contract = (((1,), (1,)), ((), ()))
+    part0 = lax.dot_general(tokx[0:rows], dn_buf[1, four:four + lat0], contract, preferred_element_type=jnp.float32)
+    part1 = lax.dot_general(tokx[0:rows], dn_buf[2, four:four + lat1], contract, preferred_element_type=jnp.float32)
+    latent = jnp.concatenate([part0, part1[:, :lora - lat0]], axis=-1)
+    inv = lax.rsqrt(jnp.mean(latent * latent, axis=-1, keepdims=True) + NORM_EPS)
+    c_new = (latent * inv * kgain_ref[...].astype(jnp.float32)).astype(jnp.bfloat16)
+    cnew_ref[...] = c_new
+    newc[...] = c_new.astype(jnp.float32)
+    key_part = jnp.concatenate([part1[:, lora - lat0:], jnp.zeros((rows, lanes - rope_dim), jnp.float32)], axis=-1)
+    k_new = rope(key_part)[:, :rope_dim].astype(jnp.bfloat16)
+    knew_ref[...] = k_new
+    newk[...] = jnp.concatenate([k_new.astype(jnp.float32), jnp.zeros((rows, lanes - rope_dim), jnp.float32)], axis=-1)
+
+    column = lax.broadcasted_iota(jnp.int32, (heads, length), 1)
+
+    def attend(seq0, keys, rope_keys):
+        scores, news = [], []
+        for s in range(8):
+            b = seq0 + s
+            q_b = qlat[b].astype(jnp.bfloat16)
+            r_b = qrot[b].astype(jnp.bfloat16)
+            score = lax.dot_general(q_b, keys(s), contract, preferred_element_type=jnp.float32)
+            score += jnp.dot(r_b[:, :rope_dim], rope_keys(s), preferred_element_type=jnp.float32)
+            scores.append(jnp.where(column < lens_ref[b], score * scale, -jnp.inf))
+            r_f = jnp.where(lax.broadcasted_iota(jnp.int32, (heads, lanes), 1) < rope_dim, r_b.astype(jnp.float32), 0.0)
+            new = jnp.sum(q_b.astype(jnp.float32) * newc[pl.ds(b, 1), :], axis=-1, keepdims=True)
+            news.append((new + jnp.sum(r_f * newk[pl.ds(b, 1), :], axis=-1, keepdims=True)) * scale)
+        scores = jnp.concatenate(scores, axis=0)
+        news = jnp.concatenate(news, axis=0)
+        top = jnp.maximum(jnp.max(scores, axis=-1, keepdims=True), news)
+        exp_cache = jnp.exp(scores - top)
+        exp_new = jnp.exp(news - top)
+        total = jnp.sum(exp_cache, axis=-1, keepdims=True) + exp_new
+        prob = (exp_cache / total).astype(jnp.bfloat16)
+        prob_new = (exp_new / total).astype(jnp.bfloat16).astype(jnp.float32)
+        for s in range(8):
+            b = seq0 + s
+            out = jnp.dot(prob[s * heads:(s + 1) * heads], keys(s), preferred_element_type=jnp.float32)
+            qlat[b] = out + prob_new[s * heads:(s + 1) * heads] * newc[pl.ds(b, 1), :]
+
+    for copy in kr_copies:
+        copy.wait()
+    for n in range(12, 16):
+        cache_copy(n).wait()
+    seqs_half = width // rope_dim
+
+    def wide_step(w, carry):
+        seq0 = wide_seqs + 8 * w
+
+        def keys(s):
+            return gu_buf[1, w, s * length:(s + 1) * length, cache_cols]
+
+        def rope_keys(s):
+            return gu_buf[2, 1, pl.ds((seq0 - seqs_half + s) * rope_dim, rope_dim), kr_cols]
+
+        attend(seq0, keys, rope_keys)
+        return carry
+
+    lax.fori_loop(0, 2, wide_step, 0)
+    hooks[1]()
+
+    def deep_step(it, carry):
+        d, i2 = it // 2, lax.rem(it, 2)
+        for k in range(2):
+            pltpu.make_async_copy(ckv_hbm.at[0:four], dn_buf.at[d, 0:four, pl.ds(pl.multiple_of((2 * i2 + k) * lora, lora), lora)], c_sem.at[2 * it + k]).wait()
+
+        def keys(s):
+            cols = pl.ds(pl.multiple_of((2 * i2 + s // 4) * lora, lora), lora)
+            return dn_buf[d, (s % 4) * length:(s % 4 + 1) * length, cols]
+
+        def rope_keys(s):
+            return gu_buf[2, it // 4, pl.ds((8 * lax.rem(it, 4) + s) * rope_dim, rope_dim), kr_cols]
+
+        attend(8 * it, keys, rope_keys)
+        hooks[2](it)
+        return carry
+
+    lax.fori_loop(0, wide_seqs // 8, deep_step, 0)
+
+    for copy in uv_copies:
+        copy.wait()
+    for h in range(heads):
+        o_lat = qlat[:, h, :].astype(jnp.bfloat16)
+        uv_head = uvbuf[(h % 2) * lora:(h % 2 + 1) * lora, (h // 2) * value_dim:(h // 2 + 1) * value_dim]
+        tokx[rows:2 * rows, h * value_dim:(h + 1) * value_dim] = jnp.dot(o_lat, uv_head, preferred_element_type=jnp.float32).astype(jnp.bfloat16)
+    parts = []
+    for w in range(2):
+        out_copies[w].wait()
+        parts.append(jnp.dot(tokx[rows:2 * rows], gu_buf[2, w, :, 0:width // 2], preferred_element_type=jnp.float32))
+    resid = hidden_ref[...].astype(jnp.float32) + jnp.concatenate(parts, axis=-1)
+    return resid.astype(jnp.bfloat16)
+
+
+def attention_kernel(*refs):
+    hidden_ref, lens_ref, again_ref, kgain_ref, ckv, krt, wq, dkvt, uk, uv, wo, resid_ref, *rest = refs
+    nothing = lambda *a: None
+    resid_ref[...] = attention_phase((hidden_ref, lens_ref, again_ref, kgain_ref, ckv, krt, wq, dkvt, uk, uv, wo, *rest), (nothing, nothing, nothing))
+
+
+def attention_layer(hidden, ckv_cache, kr_cache, seq_lens, attn_gain, kv_gain, w_q, w_dkv, w_uk, w_uv, w_o, ff):
+    rows, width = hidden.shape
+    heads, nope, lora = w_uk.shape
+    length, rope_dim = kr_cache.shape[1:]
+    vmem = pl.BlockSpec(memory_space=pltpu.VMEM)
+    hbm = pl.BlockSpec(memory_space=pl.ANY)
+    return pl.pallas_call(
+        attention_kernel,
+        out_shape=(jax.ShapeDtypeStruct((rows, width), jnp.bfloat16), jax.ShapeDtypeStruct((rows, lora), jnp.bfloat16), jax.ShapeDtypeStruct((rows, rope_dim), jnp.bfloat16)),
+        in_specs=[vmem, pl.BlockSpec(memory_space=pltpu.SMEM), vmem, vmem] + [hbm] * 7,
+        out_specs=(vmem, vmem, vmem),
+        scratch_shapes=[
+            pltpu.VMEM((128, width), jnp.bfloat16),
+            pltpu.VMEM((1024, 1536), jnp.bfloat16),
+            pltpu.VMEM((3, 2, width, ff), jnp.bfloat16),
+            pltpu.VMEM((3, ff, width), jnp.bfloat16),
+            pltpu.VMEM((rows, heads, lora), jnp.float32),
+            pltpu.VMEM((rows, heads, 128), jnp.float32),
+            pltpu.VMEM((rows, lora), jnp.float32),
+            pltpu.VMEM((rows, 128), jnp.float32),
+            pltpu.VMEM((rows, 128), jnp.float32),
+            pltpu.SemaphoreType.DMA((19,)),
+            pltpu.SemaphoreType.DMA((16,)),
+        ],
+        compiler_params=pltpu.CompilerParams(vmem_limit_bytes=67043328),
+        name='latent_attention',
+    )(hidden, seq_lens, attn_gain.reshape(1, -1), kv_gain.reshape(1, -1), ckv_cache.reshape(rows * length, lora), jnp.swapaxes(kr_cache, 1, 2).reshape(rows * rope_dim, length), w_q, w_dkv.T, w_uk.reshape(heads * nope, lora), w_uv.reshape(heads * lora, -1), w_o)
 
 
 def solution(mesh):
@@ -360,7 +535,7 @@
 
     def device_step(hidden, ckv_cache, kr_cache, seq_lens, expert_ids, attn_gain, kv_gain, moe_gain, w_q, w_dkv, w_uk, w_uv, w_o, w_router, shared_gate, shared_up, shared_down, expert_gate, expert_up, expert_down):
         capacity = max(2, 2 * hidden.shape[0] * expert_ids.shape[1] // w_router.shape[1])
-        resid_out, ckv_new, kr_new = attention_block(hidden, ckv_cache, kr_cache, seq_lens, attn_gain, kv_gain, w_q, w_dkv, w_uk, w_uv, w_o)
+        resid_out, ckv_new, kr_new = attention_layer(hidden, ckv_cache, kr_cache, seq_lens, attn_gain, kv_gain, w_q, w_dkv, w_uk, w_uv, w_o, expert_gate.shape[2])
         layer_out = moe_layer(resid_out, expert_ids, capacity, mesh.shape['dp'], moe_gain, w_router, shared_gate, shared_up, shared_down, expert_gate, expert_up, expert_down)
         return layer_out, ckv_new, kr_new
 

time: 116 us -> 97.4 us (0.84)
  matrix products: 39.4 us -> 0 us
  Pallas kernels: 65.6 us -> 89.6 us
  other arithmetic: 4.54 us -> 0 us
  local copies, waits for them, and re-layouts: 5.55 us -> 6.85 us
    dot_general x10 -> x0, matrix products: 39.4 us -> none  [the longest x1 10.2 us: attention_block(): jnp.einsum('bhc,blc->bhl', q_lat, ckv_cache, preferred_element_type=jnp.f...]
    pallas_call x0 -> x1, Pallas kernels: none -> 24.1 us  [attention_layer(): pl.pallas_call(attention_kernel, out_shape=(jax.ShapeDtypeStruct((rows, w...]
    reshape x1 -> x2, local copies, waits for them, and re-layouts: 0.61 us -> 2.52 us  [the longest x1 1.28 us: attention_layer(): attn_gain.reshape(1, -1)]
    reduce_sum x3 -> x0, other arithmetic: 1.58 us -> none  [the longest x2 1.22 us: rms_norm(): jnp.mean(vals_f32 * vals_f32, axis=-1, keepdims=True) + NORM_EPS]
    concatenate x2 -> x0, other arithmetic: 1.5 us -> none  [apply_rope(): jnp.concatenate([first_half * rope_cos - second_half * rope_sin, second_h...]
    unnamed x23 -> x2, local copies, waits for them, and re-layouts: 4.22 us -> 3.05 us
where the time goes in v1:
time: 97.4 us; the launch traced here: 97.1 us
  Pallas kernels  89.6 us (92%)
  local copies, waits for them, and re-layouts  6.85 us (7%)
    pallas_call x1, Pallas kernels, moe_layer(): pl.pallas_call(functools.partial(moe_kernel, dims), out_shape=jax.ShapeDt...  65.5 us
    pallas_call x1, Pallas kernels, attention_layer(): pl.pallas_call(attention_kernel, out_shape=(jax.ShapeDtypeStruct((rows, w...  24.1 us
    unnamed x2, local copies, waits for them, and re-layouts  3.05 us

profile of v1, /device:TPU:113, one launch (start us, length us, event | category | flops | bytes accessed | tf_op | source)
XLA Modules:
  0.0 97.1 jit_solution(266942166831735942)
XLA Ops:
  0.6 1.2 %reshape.28.refs_3_ = bf16[1,512]{1,0:T(2,128)(2,1)} reshape(bf16[512]{0:T(512)(128)(2,1)} %param.26) | data formatting | bytes 2048 | tf_op jit(solution)/shard_map/reshape | solution.py:528
  1.9 1.3 %reshape.27.refs_2_ = bf16[1,2048]{1,0:T(2,128)(2,1)} reshape(bf16[2048]{0:T(1024)(128)(2,1)} %param.25) | data formatting | bytes 8192 | tf_op jit(solution)/shard_map/reshape | solution.py:528
  3.2 1.3 %reshape.33.gain_ref = bf16[1,2048]{1,0:T(2,128)(2,1)} reshape(bf16[2048]{0:T(1024)(128)(2,1)} %param.27) | data formatting | bytes 8192 | tf_op jit(solution)/shard_map/reshape | solution.py:305
  4.4 1.4 %copy.23.ids_ref = s32[64,6]{1,0:T(8,128)} copy(s32[64,6]{0,1:T(8,128)} %param.24) | data formatting | bytes 3072 | tf_op args[4]
  5.8 24.1 %latent_attention.1 = (bf16[64,2048]{1,0:T(8,128)(2,1)}, bf16[64,512]{1,0:T(8,128)(2,1)}, bf16[64,64]{1,0:T(8,128)(2,1)}) custom-call(bf16[64,2048]{1,0:T(8,128)(2,1)} %refs_0_.1, s32[64]{0:T(128)} %refs_1_.1, bf16[1,2048]{1,0:T(2,128)(2,1)} %reshape.27.refs_2_, bf16[1,512]{1,0:T(2,128)(2,1)} %reshape.28.refs_3_, bf16[16384,512]{1,0:T(8,128)(2,1)} %bitcast.8, ...), custom_call_target="tpu_custom_call" | custom-call | tf_op jit(solution)/shard_map/latent_attention/pallas_call | solution.py:508
  30.0 65.5 %moe_layer.1 = bf16[64,2048]{1,0:T(8,128)(2,1)} custom-call(bf16[64,2048]{1,0:T(8,128)(2,1)} %get-tuple-element.6.resid_ref, s32[64,6]{1,0:T(8,128)} %copy.23.ids_ref, bf16[1,2048]{1,0:T(2,128)(2,1)} %reshape.33.gain_ref, bf16[64,2048]{1,0:T(8,128)(2,1)} %bitcast.13, bf16[2048,2816]{1,0:T(8,128)(2,1)} %sgate_hbm.1, bf16[2048,2816]{1,0:T(8,128)(2,1)} %sup_hbm.1, ...), custom_call_target="tpu_custom_call" | custom-call | tf_op jit(solution)/shard_map/moe_layer/pallas_call | solution.py:280
  95.5 1.7 %copy.25 = bf16[64,2048]{1,0:T(8,128)(2,1)} copy(bf16[64,2048]{1,0:T(8,128)(2,1)} %moe_layer.1) | data formatting | bytes 524288

commit v2 on v0

v2 whole, which is shorter than its diff:
```python
import functools
import math

import jax
import jax.numpy as jnp
from jax import lax
from jax.experimental import pallas as pl
from jax.experimental.pallas import tpu as pltpu
from jax.sharding import PartitionSpec as P

NORM_EPS = 1e-6
ROPE_THETA = 10000.0


MESH_ID = pl.DeviceIdType.MESH


def attention_phase(refs, hooks):
    (hidden_hbm, hidden_ref, lens_ref, again_ref, kgain_ref, ckv_hbm, krt_hbm, wq_hbm, dkvt_hbm, uk_hbm, uv_hbm, wo_hbm, cnew_ref, knew_ref,
     tokx, uvbuf, gu_buf, dn_buf, qlat, qrot, newc, newk, pos, a_sem, c_sem) = refs
    rows, width = hidden_ref.shape
    lora = qlat.shape[-1]
    heads = qlat.shape[1]
    rope_dim = krt_hbm.shape[0] // rows
    length = krt_hbm.shape[1]
    nope = uk_hbm.shape[0] // heads
    head_dim = nope + rope_dim
    qcols = wq_hbm.shape[1] // 4
    four = 4 * length
    value_dim = uv_hbm.shape[-1]
    scale = head_dim ** -0.5
    lanes = 128
    lat0 = dn_buf.shape[1] - four
    lat1 = dkvt_hbm.shape[0] - lat0
    cache_cols = slice(qcols, qcols + lora)
    kr_cols = slice(width // 2, width // 2 + length)

    def query_copy(i):
        return pltpu.make_async_copy(wq_hbm.at[:, i * qcols:(i + 1) * qcols], gu_buf.at[i // 2, i % 2, :, 0:qcols], a_sem.at[i])

    latent_copies = [
        pltpu.make_async_copy(dkvt_hbm.at[0:lat0], dn_buf.at[1, four:four + lat0], a_sem.at[4]),
        pltpu.make_async_copy(dkvt_hbm.at[lat0:lat0 + lat1], dn_buf.at[2, four:four + lat1], a_sem.at[5]),
    ]
    uk_copy = pltpu.make_async_copy(uk_hbm, gu_buf.at[0, 1, :, cache_cols], a_sem.at[6])
    kr_copies = [pltpu.make_async_copy(krt_hbm.at[w * width:(w + 1) * width], gu_buf.at[2, w, :, kr_cols], a_sem.at[7 + w]) for w in range(2)]
    out_copies = [pltpu.make_async_copy(wo_hbm.at[:, w * (width // 2):(w + 1) * (width // 2)], gu_buf.at[2, w, :, 0:width // 2], a_sem.at[9 + w]) for w in range(2)]
    uv_copies = [pltpu.make_async_copy(uv_hbm.at[i], uvbuf.at[:, :, :, i * value_dim:(i + 1) * value_dim], a_sem.at[11 + i]) for i in range(heads // 2)]
    wide_seqs = 48

    def cache_copy(n):
        if n >= 12:
            w, r = (n - 12) // 2, n % 2
            return pltpu.make_async_copy(ckv_hbm.at[n * four:(n + 1) * four], gu_buf.at[1, w, r * four:(r + 1) * four, cache_cols], c_sem.at[n])
        return pltpu.make_async_copy(ckv_hbm.at[n * four:(n + 1) * four], dn_buf.at[n // 4, 0:four, (n % 4) * lora:(n % 4 + 1) * lora], c_sem.at[n])

    hidden_copy = pltpu.make_async_copy(hidden_hbm, hidden_ref, a_sem.at[19])
    hidden_copy.start()
    query_copy(0).start()
    for copy in latent_copies:
        copy.start()
    uk_copy.start()
    for i in range(1, 4):
        query_copy(i).start()

    lane = lax.broadcasted_iota(jnp.int32, (rows, lanes), 1)
    hidden_copy.wait()
    hidden = hidden_ref[...].astype(jnp.float32)
    inv = lax.rsqrt(jnp.mean(hidden * hidden, axis=-1, keepdims=True) + NORM_EPS)
    tokx[0:rows] = (hidden * inv * again_ref[...].astype(jnp.float32)).astype(jnp.bfloat16)
    for b in range(rows):
        pos[b:b + 1, :] = jnp.full((1, lanes), lens_ref[b], jnp.int32).astype(jnp.float32)
    quarter = lax.rem(lane, rope_dim // 2).astype(jnp.float32)
    angle = pos[...] * jnp.exp(quarter * (-2.0 / rope_dim * math.log(ROPE_THETA)))
    rope_cos = jnp.cos(angle)
    low_half = lax.rem(lane, rope_dim) < rope_dim // 2
    rope_sin = jnp.where(low_half, -jnp.sin(angle), jnp.sin(angle))

    def rope(value):
        swapped = jnp.where(low_half, pltpu.roll(value, lanes - rope_dim // 2, 1), pltpu.roll(value, rope_dim // 2, 1))
        return value * rope_cos + swapped * rope_sin

    first_half = lane < rope_dim

    def row_of(h):
        return (h % 2) * (heads // 2) + h // 2

    for i in range(4):
        query_copy(i).wait()
        q_cols = jnp.dot(tokx[0:rows], gu_buf[i // 2, i % 2, :, 0:qcols], preferred_element_type=jnp.float32)
        q_cols = q_cols.astype(jnp.bfloat16).astype(jnp.float32)
        if i == 0:
            for n in range(12, 16):
                cache_copy(n).start()
            for copy in kr_copies:
                copy.start()
            uk_copy.wait()
        if i == 1:
            for n in range(4):
                cache_copy(n).start()
        for pair in range(qcols // (2 * head_dim)):
            base = pair * 2 * head_dim
            tile0, tile1, tile2 = (q_cols[:, base + k * lanes:base + (k + 1) * lanes] for k in range(3))
            head = i * (qcols // head_dim) + 2 * pair
            nopes = (tile0, pltpu.roll(jnp.where(first_half, tile2, tile1), lanes // 2, 1))
            turned = rope(jnp.where(first_half, tile1, tile2))
            qrot[:, head // 2, :] = turned
            for odd in range(2):
                h = head + odd
                uk_head = gu_buf[0, 1, h * nope:(h + 1) * nope, cache_cols]
                qlat[:, row_of(h), :] = jnp.dot(nopes[odd].astype(jnp.bfloat16), uk_head, preferred_element_type=jnp.float32)
    for n in range(4, 12):
        cache_copy(n).start()
    for copy in uv_copies + out_copies:
        copy.start()
    hooks[0]()

    for copy in latent_copies:
        copy.wait()
    contract = (((1,), (1,)), ((), ()))
    part0 = lax.dot_general(tokx[0:rows], dn_buf[1, four:four + lat0], contract, preferred_element_type=jnp.float32)
    part1 = lax.dot_general(tokx[0:rows], dn_buf[2, four:four + lat1], contract, preferred_element_type=jnp.float32)
    latent = jnp.concatenate([part0, part1[:, :lora - lat0]], axis=-1)
    inv = lax.rsqrt(jnp.mean(latent * latent, axis=-1, keepdims=True) + NORM_EPS)
    c_new = (latent * inv * kgain_ref[...].astype(jnp.float32)).astype(jnp.bfloat16)
    cnew_ref[...] = c_new
    newc[...] = c_new.astype(jnp.float32)
    key_part = jnp.concatenate([part1[:, lora - lat0:], jnp.zeros((rows, lanes - rope_dim), jnp.float32)], axis=-1)
    k_new = rope(key_part)[:, :rope_dim].astype(jnp.bfloat16)
    knew_ref[...] = k_new
    newk[...] = jnp.concatenate([k_new.astype(jnp.float32), jnp.zeros((rows, lanes - rope_dim), jnp.float32)], axis=-1)

    column = lax.broadcasted_iota(jnp.int32, (heads, length), 1)

    def attend(seq0, keys, rope_keys):
        scores, news = [], []
        for s in range(8):
            b = seq0 + s
            q_b = qlat[b].astype(jnp.bfloat16)
            pairs = qrot[b]
            r_b = jnp.concatenate([pairs, pltpu.roll(pairs, lanes // 2, 1)], axis=0).astype(jnp.bfloat16)
            score = lax.dot_general(q_b, keys(s), contract, preferred_element_type=jnp.float32)
            score += jnp.dot(r_b[:, :rope_dim], rope_keys(s), preferred_element_type=jnp.float32)
            scores.append(jnp.where(column < lens_ref[b], score * scale, -jnp.inf))
            r_f = jnp.where(lax.broadcasted_iota(jnp.int32, (heads, lanes), 1) < rope_dim, r_b.astype(jnp.float32), 0.0)
            new = jnp.sum(q_b.astype(jnp.float32) * newc[pl.ds(b, 1), :], axis=-1, keepdims=True)
            news.append((new + jnp.sum(r_f * newk[pl.ds(b, 1), :], axis=-1, keepdims=True)) * scale)
        scores = jnp.concatenate(scores, axis=0)
        news = jnp.concatenate(news, axis=0)
        top = jnp.maximum(jnp.max(scores, axis=-1, keepdims=True), news)
        exp_cache = jnp.exp(scores - top)
        exp_new = jnp.exp(news - top)
        total = jnp.sum(exp_cache, axis=-1, keepdims=True) + exp_new
        prob = (exp_cache / total).astype(jnp.bfloat16)
        prob_new = (exp_new / total).astype(jnp.bfloat16).astype(jnp.float32)
        for s in range(8):
            b = seq0 + s
            out = jnp.dot(prob[s * heads:(s + 1) * heads], keys(s), preferred_element_type=jnp.float32)
            qlat[b] = out + prob_new[s * heads:(s + 1) * heads] * newc[pl.ds(b, 1), :]

    for copy in kr_copies:
        copy.wait()
    for n in range(12, 16):
        cache_copy(n).wait()
    seqs_half = width // rope_dim

    def wide_step(w, carry):
        seq0 = wide_seqs + 8 * w

        def keys(s):
            return gu_buf[1, w, s * length:(s + 1) * length, cache_cols]

        def rope_keys(s):
            return gu_buf[2, 1, pl.ds((seq0 - seqs_half + s) * rope_dim, rope_dim), kr_cols]

        attend(seq0, keys, rope_keys)
        return carry

    lax.fori_loop(0, 2, wide_step, 0)
    hooks[1]()

    def deep_step(it, carry):
        d, i2 = it // 2, lax.rem(it, 2)
        for k in range(2):
            pltpu.make_async_copy(ckv_hbm.at[0:four], dn_buf.at[d, 0:four, pl.ds(pl.multiple_of((2 * i2 + k) * lora, lora), lora)], c_sem.at[2 * it + k]).wait()

        def keys(s):
            cols = pl.ds(pl.multiple_of((2 * i2 + s // 4) * lora, lora), lora)
            return dn_buf[d, (s % 4) * length:(s % 4 + 1) * length, cols]

        def rope_keys(s):
            return gu_buf[2, it // 4, pl.ds((8 * lax.rem(it, 4) + s) * rope_dim, rope_dim), kr_cols]

        attend(8 * it, keys, rope_keys)
        hooks[2](it)
        return carry

    lax.fori_loop(0, wide_seqs // 8, deep_step, 0)

    for copy in uv_copies:
        copy.wait()
    for h in range(heads):
        o_lat = qlat[:, row_of(h), :].astype(jnp.bfloat16)
        uv_half = uvbuf.shape[0] // 2
        uv_head = uvbuf[(h % 2) * uv_half:(h % 2 + 1) * uv_half, :, :, (h // 2) * value_dim:(h // 2 + 1) * value_dim].reshape(lora, value_dim)
        tokx[rows:2 * rows, h * value_dim:(h + 1) * value_dim] = jnp.dot(o_lat, uv_head, preferred_element_type=jnp.float32).astype(jnp.bfloat16)
    parts = []
    for w in range(2):
        out_copies[w].wait()
        parts.append(jnp.dot(tokx[rows:2 * rows], gu_buf[2, w, :, 0:width // 2], preferred_element_type=jnp.float32))
    hooks[3]()
    resid = hidden_ref[...].astype(jnp.float32) + jnp.concatenate(parts, axis=-1)
    return resid.astype(jnp.bfloat16)


def silu(value):
    return value * (1.0 / (1.0 + jnp.exp(-value)))


def layer_kernel(dims, hidden_hbm, lens_ref, ids_ref, again_ref, kgain_ref, gain_ref, router_ref, ckv_hbm, krt_hbm, wq_hbm, dkvt_hbm, uk_hbm, uv_hbm, wo_hbm,
                 sgate_hbm, sup_hbm, sdown_hbm, egate_hbm, eup_hbm, edown_hbm, out_ref, cnew_ref, knew_ref,
                 ublk, tokx, midx, send, recv, acc, table, tail, gu_buf, dn_buf, qlat, qrot, newc, newk,
                 gu_sem, dn_sem, us_sem, ur_sem, ys_sem, yr_sem, a_sem, c_sem):
    group, experts_dev, experts, cap, depth, dp_axis = dims
    rows, width = hidden_hbm.shape
    half = rows // 2
    ff = gu_buf.shape[-1]
    n_shared = sgate_hbm.shape[-1] // ff
    steps = experts_dev + n_shared
    slot16 = 16
    slots = group * slot16
    main = send.shape[-1]
    blk = main // 3
    top_k = ids_ref.shape[0]
    lag = 4
    lanes = 128
    me = lax.axis_index(dp_axis)
    chips = group // 2
    core = lax.rem(me, 2)
    chip = me // 2
    partner = chip * 2 + (1 - core)
    left = lax.rem(chip + chips - 1, chips) * 2 + core
    right = lax.rem(chip + 1, chips) * 2 + core
    far = lax.rem(chip + 2, chips) * 2 + core

    def routed(step):
        return (step >= 1) & (step <= experts_dev)

    def either(condition, action_a, action_b):
        if isinstance(condition, bool):
            (action_a if condition else action_b)()
        else:
            pl.when(condition)(action_a)
            pl.when(jnp.logical_not(condition))(action_b)

    def weights_gu(step, which, hbm, shared_hbm, action):
        slot = step % depth if isinstance(step, int) else lax.rem(step, depth)

        def own():
            getattr(pltpu.make_async_copy(hbm.at[step - 1], gu_buf.at[slot, which], gu_sem.at[slot, which]), action)()

        def shared():
            start = step // (steps - 1) * ff
            cols = pl.ds(start if isinstance(step, int) else pl.multiple_of(start, 128), ff)
            getattr(pltpu.make_async_copy(shared_hbm.at[:, cols], gu_buf.at[slot, which], gu_sem.at[slot, which]), action)()

        either(routed(step), own, shared)

    def weights_dn(step, action):
        slot = step % depth if isinstance(step, int) else lax.rem(step, depth)

        def own():
            getattr(pltpu.make_async_copy(edown_hbm.at[step - 1], dn_buf.at[slot], dn_sem.at[slot]), action)()

        def shared():
            start = step // (steps - 1) * ff
            cols = pl.ds(start if isinstance(step, int) else pl.multiple_of(start, 128), ff)
            getattr(pltpu.make_async_copy(sdown_hbm.at[cols], dn_buf.at[slot], dn_sem.at[slot]), action)()

        either(routed(step), own, shared)

    def fetch(step):
        weights_gu(step, 0, egate_hbm, sgate_hbm, "start")
        weights_gu(step, 1, eup_hbm, sup_hbm, "start")

    barrier = pltpu.get_barrier_semaphore()
    for k in range(1, group):
        pl.semaphore_signal(barrier, inc=1, device_id={dp_axis: lax.rem(me + k, group)}, device_id_type=MESH_ID)

    def freed_deep(it):
        for d in range(depth):
            @pl.when(it == 2 * d + 1)
            def _():
                weights_dn(d, "start")

    hooks = (lambda: fetch(0), lambda: fetch(1), freed_deep, lambda: fetch(2))
    resid = attention_phase((hidden_hbm, out_ref, lens_ref, again_ref, kgain_ref, ckv_hbm, krt_hbm, wq_hbm, dkvt_hbm, uk_hbm, uv_hbm, wo_hbm, cnew_ref, knew_ref,
                             tokx, send, gu_buf, dn_buf, qlat, qrot, newc, newk, acc.at[:, 0:128], a_sem, c_sem), hooks)

    resid = resid.astype(jnp.float32)
    inv = lax.rsqrt(jnp.mean(resid * resid, axis=-1, keepdims=True) + NORM_EPS)
    u = (resid * inv * gain_ref[...].astype(jnp.float32)).astype(jnp.bfloat16)
    expert_i = lax.broadcasted_iota(jnp.int32, (lanes, rows), 0)
    picked = ids_ref[0:1, :] == expert_i
    for k in range(1, top_k):
        picked = picked | (ids_ref[k:k + 1, :] == expert_i)
    tok_a = lax.broadcasted_iota(jnp.int32, (rows, rows), 0)
    tok_b = lax.broadcasted_iota(jnp.int32, (rows, rows), 1)
    before = jnp.where(tok_a < tok_b, 1.0, 0.0).astype(jnp.bfloat16)
    rank = jnp.dot(jnp.where(picked, 1.0, 0.0).astype(jnp.bfloat16), before, preferred_element_type=jnp.float32)
    codes_t = jnp.where(picked, rank, -1.0).astype(jnp.bfloat16)
    same = jnp.where(tok_a == tok_b, 1.0, 0.0).astype(jnp.bfloat16)
    codes = lax.dot_general(same, codes_t, (((1,), (1,)), ((), ())), preferred_element_type=jnp.float32).astype(jnp.bfloat16)
    for h in range(2):
        ublk[me, h, :, :width] = u[h * half:(h + 1) * half]
        ublk[me, h, :, width:] = codes[h * half:(h + 1) * half]
    logits = lax.dot_general(u, router_ref[...], (((1,), (1,)), ((), ())), preferred_element_type=jnp.float32)
    logits = logits - jnp.max(logits, axis=-1, keepdims=True)
    expl = jnp.exp(logits)
    prob = expl / jnp.sum(expl, axis=-1, keepdims=True)
    prob = jnp.concatenate([prob, jnp.zeros((rows, lanes - experts), jnp.float32)], axis=-1)
    p0 = prob.astype(jnp.bfloat16)
    rest = prob - p0.astype(jnp.float32)
    p1 = rest.astype(jnp.bfloat16)
    p2 = (rest - p1.astype(jnp.float32)).astype(jnp.bfloat16)
    table[0] = codes
    table[1] = p0
    table[2] = p1
    table[3] = p2
    acc[...] = resid

    pl.semaphore_wait(barrier, group - 1)

    def block_copy(block, h, dest, sem_no):
        return pltpu.make_async_remote_copy(src_ref=ublk.at[block, h], dst_ref=ublk.at[block, h], send_sem=us_sem.at[sem_no], recv_sem=ur_sem.at[block, h], device_id={dp_axis: dest}, device_id_type=MESH_ID)

    def crossed(block):
        return lax.rem(block + 1 - 2 * core + group, group)

    first_sends = ((me, 0, right), (me, 1, left), (me, 1, right), (me, 0, left), (me, 0, partner), (me, 1, partner))
    relays = ((left, 0, right), (left, 0, partner), (right, 1, left), (right, 1, partner), (left, 1, partner), (right, 0, partner), (far, 0, partner), (far, 1, partner))
    all_sends = first_sends + relays

    def send_block(n):
        block, h, dest = all_sends[n]
        block_copy(block, h, dest, n).start()

    def arrived(block, h):
        block_copy(block, h, partner, 0).wait_recv()

    for n in range(len(first_sends)):
        send_block(n)

    def relay():
        seen = set()
        for n in range(len(first_sends), len(all_sends)):
            block, h, _ = all_sends[n]
            if (id(block), h) not in seen:
                seen.add((id(block), h))
                arrived(block, h)
            send_block(n)
        for block in (partner, crossed(left), crossed(right), crossed(far)):
            for h in range(2):
                arrived(block, h)

    row_i = lax.broadcasted_iota(jnp.int32, (lanes, slots), 0)
    col_i = lax.broadcasted_iota(jnp.int32, (lanes, slots), 1)

    def return_copy(step, dest):
        return pltpu.make_async_remote_copy(src_ref=send.at[step, dest], dst_ref=recv.at[step, me], send_sem=ys_sem.at[step, dest], recv_sem=yr_sem.at[step, me], device_id={dp_axis: dest}, device_id_type=MESH_ID)

    def arrival(step, source):
        return pltpu.make_async_remote_copy(src_ref=send.at[step, source], dst_ref=recv.at[step, source], send_sem=ys_sem.at[step, source], recv_sem=yr_sem.at[step, source], device_id={dp_axis: source}, device_id_type=MESH_ID)

    def gather_rows(expert):
        pick = (row_i == me * experts_dev + expert).astype(jnp.float32).astype(jnp.bfloat16)
        code_all = ublk[:, :, :, width:].reshape(group * rows, lanes)
        code_b = jnp.dot(code_all, pick, preferred_element_type=jnp.float32)
        tok = lax.broadcasted_iota(jnp.int32, (group * rows, slots), 0)
        col = lax.broadcasted_iota(jnp.int32, (group * rows, slots), 1)
        hit = (code_b == lax.rem(col, slot16).astype(jnp.float32)) & (tok // rows == col // slot16)
        place = jnp.where(hit, 1.0, 0.0).astype(jnp.bfloat16)
        for c0 in range(0, width, 512):
            rows_u = ublk[:, :, :, c0:c0 + 512].reshape(group * rows, 512)
            picked_rows = lax.dot_general(place, rows_u, (((0,), (0,)), ((), ())), preferred_element_type=jnp.float32)
            tokx[:, c0:c0 + 512] = picked_rows.astype(jnp.bfloat16)

    def pack_block(y_main, q):
        y_main = y_main.reshape(group, 2, 8, blk)
        y_tail = tail[...].reshape(group, 2, 8, blk)
        sub = lax.broadcasted_iota(jnp.int32, (group, 8, blk), 1)
        part = y_tail[:, 1 if q == 2 else 0]
        if q != 1:
            part = pltpu.roll(part.reshape(group * 8, blk).reshape(group, 8, blk), 4, 1)
        low = jnp.where(sub >= 4, part, y_main[:, 1])
        return jnp.concatenate([y_main[:, 0], low], axis=1).astype(jnp.bfloat16)

    def combine(step):
        for k in range(1, group):
            arrival(step, lax.rem(me + k, group)).wait_recv()
        spread = (row_i == (col_i // slot16) * experts_dev + step).astype(jnp.float32).astype(jnp.bfloat16)
        wide = jnp.dot(table[...].reshape(4 * rows, lanes), spread, preferred_element_type=jnp.float32)
        code_b = wide[:rows]
        slot_i = lax.rem(lax.broadcasted_iota(jnp.int32, (rows, slots), 1), slot16)
        slot_f = slot_i.astype(jnp.float32)
        for q in range(3):
            hits = [code_b == slot_f, (slot_i >= cap) & (code_b == slot_f - cap + 4 * q)]
            lhs = jnp.concatenate([jnp.where(hit, wide[p * rows:(p + 1) * rows], 0.0) for hit in hits for p in (1, 2, 3)], axis=0).astype(jnp.bfloat16)
            y_blk = recv[step, :, :, q * blk:(q + 1) * blk].reshape(slots, blk)
            res = jnp.dot(lhs, y_blk, preferred_element_type=jnp.float32)
            acc[:, q * blk:(q + 1) * blk] += res[:rows] + (res[rows:2 * rows] + res[2 * rows:3 * rows])
            acc[:, main:] += res[3 * rows:4 * rows] + (res[4 * rows:5 * rows] + res[5 * rows:])

    def one_step(step, carry):
        slot = lax.rem(step, depth)
        expert = step - 1
        is_routed = routed(step)

        @pl.when(step == 1)
        def _():
            relay()

        @pl.when(is_routed)
        def _():
            gather_rows(expert)

        @pl.when(jnp.logical_not(is_routed))
        def _():
            tokx[:rows] = ublk[me, :, :, :width].reshape(rows, width)
            tokx[rows:] = jnp.zeros((slots - rows, width), jnp.bfloat16)

        weights_gu(step, 0, egate_hbm, sgate_hbm, "wait")
        weights_gu(step, 1, eup_hbm, sup_hbm, "wait")
        for c0 in range(0, ff, 512):
            c1 = min(c0 + 512, ff)
            gate_act = jnp.dot(tokx[...], gu_buf[slot, 0, :, c0:c1], preferred_element_type=jnp.float32)
            up_act = jnp.dot(tokx[...], gu_buf[slot, 1, :, c0:c1], preferred_element_type=jnp.float32)
            midx[:, c0:c1] = (silu(gate_act) * up_act).astype(jnp.bfloat16)

        @pl.when(step + depth < steps)
        def _():
            fetch(step + depth)

        weights_dn(step, "wait")
        tail[...] = jnp.dot(midx[...], dn_buf[slot, :, main:], preferred_element_type=jnp.float32)

        @pl.when(jnp.logical_not(is_routed))
        def _():
            acc[:, main:] += tail[:rows]

        for q in range(3):
            y_main = jnp.dot(midx[...], dn_buf[slot, :, q * blk:(q + 1) * blk], preferred_element_type=jnp.float32)

            @pl.when(is_routed)
            def _():
                send[expert, :, :, q * blk:(q + 1) * blk] = pack_block(y_main, q)

            @pl.when(jnp.logical_not(is_routed))
            def _():
                acc[:, q * blk:(q + 1) * blk] += y_main[:rows]

        @pl.when(step + depth < steps)
        def _():
            weights_dn(step + depth, "start")

        @pl.when(is_routed)
        def _():
            recv[expert, me] = send[expert, me]
            for k in (4, 3, 5, 2, 6, 1, 7):
                return_copy(expert, lax.rem(me + k, group)).start()

        @pl.when(expert >= lag)
        def _():
            combine(expert - lag)

        return carry

    lax.fori_loop(0, steps, one_step, 0)

    def last_combine(step, carry):
        combine(step)
        return carry

    lax.fori_loop(steps - 1 - lag, experts_dev, last_combine, 0)
    out_ref[...] = acc[...].astype(out_ref.dtype)

    for n, (block, h, dest) in enumerate(all_sends):
        block_copy(block, h, dest, n).wait_send()

    def drain(step, carry):
        for k in range(1, group):
            return_copy(step, lax.rem(me + k, group)).wait_send()
        return carry

    lax.fori_loop(0, experts_dev, drain, 0)


def layer(group, cap, hidden, ckv_cache, kr_cache, seq_lens, expert_ids, attn_gain, kv_gain, moe_gain, w_q, w_dkv, w_uk, w_uv, w_o, w_router, shared_gate, shared_up, shared_down, expert_gate, expert_up, expert_down):
    rows, width = hidden.shape
    heads, nope, lora = w_uk.shape
    length, rope_dim = kr_cache.shape[1:]
    experts_dev, _, ff = expert_gate.shape
    experts = w_router.shape[1]
    depth = 3
    main = 3 * width // 4
    slots = group * 16
    dims = (group, experts_dev, experts, cap, depth, 'dp')
    vmem = pl.BlockSpec(memory_space=pltpu.VMEM)
    hbm = pl.BlockSpec(memory_space=pl.ANY)
    return pl.pallas_call(
        functools.partial(layer_kernel, dims),
        out_shape=(jax.ShapeDtypeStruct((rows, width), jnp.bfloat16), jax.ShapeDtypeStruct((rows, lora), jnp.bfloat16), jax.ShapeDtypeStruct((rows, rope_dim), jnp.bfloat16)),
        in_specs=[hbm, pl.BlockSpec(memory_space=pltpu.SMEM)] + [vmem] * 5 + [hbm] * 13,
        out_specs=(vmem, vmem, vmem),
        scratch_shapes=[
            pltpu.VMEM((group, 2, rows // 2, width + 128), jnp.bfloat16),
            pltpu.VMEM((slots, width), jnp.bfloat16),
            pltpu.VMEM((slots, ff), jnp.bfloat16),
            pltpu.VMEM((experts_dev, group, 16, main), jnp.bfloat16),
            pltpu.VMEM((experts_dev, group, 16, main), jnp.bfloat16),
            pltpu.VMEM((rows, width), jnp.float32),
            pltpu.VMEM((4, rows, 128), jnp.bfloat16),
            pltpu.VMEM((slots, width - main), jnp.float32),
            pltpu.VMEM((depth, 2, width, ff), jnp.bfloat16),
            pltpu.VMEM((depth, ff, width), jnp.bfloat16),
            pltpu.VMEM((rows, heads, lora), jnp.float32),
            pltpu.VMEM((rows, heads // 2, 128), jnp.float32),
            pltpu.VMEM((rows, lora), jnp.float32),
            pltpu.VMEM((rows, 128), jnp.float32),
            pltpu.SemaphoreType.DMA((depth, 2)),
            pltpu.SemaphoreType.DMA((depth,)),
            pltpu.SemaphoreType.DMA((14,)),
            pltpu.SemaphoreType.DMA((group, 2)),
            pltpu.SemaphoreType.DMA((experts_dev, group)),
            pltpu.SemaphoreType.DMA((experts_dev, group)),
            pltpu.SemaphoreType.DMA((20,)),
            pltpu.SemaphoreType.DMA((16,)),
        ],
        compiler_params=pltpu.CompilerParams(collective_id=0, has_side_effects=True, vmem_limit_bytes=67043328),
        name='decoder_layer',
    )(hidden, seq_lens, expert_ids.T, attn_gain.reshape(1, -1), kv_gain.reshape(1, -1), moe_gain.reshape(1, -1), w_router.T,
      ckv_cache.reshape(rows * length, lora), jnp.swapaxes(kr_cache, 1, 2).reshape(rows * rope_dim, length), w_q, w_dkv.T, w_uk.reshape(heads * nope, lora),
      w_uv.reshape(heads // 2, experts_dev, group, 16, -1), w_o, shared_gate, shared_up, shared_down, expert_gate, expert_up, expert_down)


def solution(mesh):
    row_spec = P(('rep', 'dp'))
    full_spec = P()
    expert_spec = P('dp')

    def device_step(hidden, ckv_cache, kr_cache, seq_lens, expert_ids, attn_gain, kv_gain, moe_gain, w_q, w_dkv, w_uk, w_uv, w_o, w_router, shared_gate, shared_up, shared_down, expert_gate, expert_up, expert_down):
        capacity = max(2, 2 * hidden.shape[0] * expert_ids.shape[1] // w_router.shape[1])
        return layer(mesh.shape['dp'], capacity, hidden, ckv_cache, kr_cache, seq_lens, expert_ids, attn_gain, kv_gain, moe_gain, w_q, w_dkv, w_uk, w_uv, w_o, w_router, shared_gate, shared_up, shared_down, expert_gate, expert_up, expert_down)

    in_specs = (row_spec,) * 5 + (full_spec,) * 12 + (expert_spec,) * 3
    return jax.shard_map(device_step, mesh=mesh, in_specs=in_specs, out_specs=(row_spec, row_spec, row_spec), check_vma=False)
```

time: 116 us -> 93.6 us (0.81)
  matrix products: 39.4 us -> 0 us
  Pallas kernels: 65.6 us -> 84.4 us
  other arithmetic: 4.54 us -> 0 us
  local copies, waits for them, and re-layouts: 5.55 us -> 8.3 us
    dot_general x10 -> x0, matrix products: 39.4 us -> none  [the longest x1 10.2 us: attention_block(): jnp.einsum('bhc,blc->bhl', q_lat, ckv_cache, preferred_element_type=jnp.f...]
    pallas_call x1, Pallas kernels: 65.6 us -> 84.4 us  [layer(): pl.pallas_call(functools.partial(layer_kernel, dims), out_shape=(jax.Shap...]
    reshape x2 -> x3, local copies, waits for them, and re-layouts: 1.21 us -> 3.84 us  [the longest x1 1.29 us: layer(): attn_gain.reshape(1, -1)]
    reduce_sum x3 -> x0, other arithmetic: 1.58 us -> none  [the longest x2 1.22 us: rms_norm(): jnp.mean(vals_f32 * vals_f32, axis=-1, keepdims=True) + NORM_EPS]
    concatenate x2 -> x0, other arithmetic: 1.5 us -> none  [apply_rope(): jnp.concatenate([first_half * rope_cos - second_half * rope_sin, second_h...]
    unnamed x23 -> x3, local copies, waits for them, and re-layouts: 4.22 us -> 4.46 us
where the time goes in v2:
time: 93.6 us; the launch traced here: 93.3 us
  Pallas kernels  84.4 us (90%)
  local copies, waits for them, and re-layouts  8.3 us (9%)
    pallas_call x1, Pallas kernels, layer(): pl.pallas_call(functools.partial(layer_kernel, dims), out_shape=(jax.Shap...  84.4 us
    unnamed x3, local copies, waits for them, and re-layouts  4.46 us

profile of v2, /device:TPU:113, one launch (start us, length us, event | category | flops | bytes accessed | tf_op | source)
XLA Modules:
  0.0 93.3 jit_solution(11057893633582547004)
XLA Ops:
  0.6 1.3 %reshape.28.kgain_ref = bf16[1,512]{1,0:T(2,128)(2,1)} reshape(bf16[512]{0:T(512)(128)(2,1)} %param.26) | data formatting | bytes 2048 | tf_op jit(solution)/shard_map/reshape | solution.py:541
  1.9 1.3 %reshape.27.again_ref = bf16[1,2048]{1,0:T(2,128)(2,1)} reshape(bf16[2048]{0:T(1024)(128)(2,1)} %param.25) | data formatting | bytes 8192 | tf_op jit(solution)/shard_map/reshape | solution.py:541
  3.2 1.3 %reshape.29.gain_ref = bf16[1,2048]{1,0:T(2,128)(2,1)} reshape(bf16[2048]{0:T(1024)(128)(2,1)} %param.27) | data formatting | bytes 8192 | tf_op jit(solution)/shard_map/reshape | solution.py:541
  4.5 84.4 %decoder_layer.1 = (bf16[64,2048]{1,0:T(8,128)(2,1)}, bf16[64,512]{1,0:T(8,128)(2,1)}, bf16[64,64]{1,0:T(8,128)(2,1)}) custom-call(bf16[64,2048]{1,0:T(8,128)(2,1)} %hidden_hbm.1, s32[64]{0:T(128)} %lens_ref.1, s32[6,64]{1,0:T(8,128)} %bitcast.15, bf16[1,2048]{1,0:T(2,128)(2,1)} %reshape.27.again_ref, bf16[1,512]{1,0:T(2,128)(2,1)} %reshape.28.kgain_ref, ...), custom_call_target="tpu_custom_call" | custom-call | tf_op jit(solution)/shard_map/decoder_layer/pallas_call | solution.py:510
  88.9 1.7 %copy.26 = bf16[64,2048]{1,0:T(8,128)(2,1)} copy(bf16[64,2048]{1,0:T(8,128)(2,1)} %get-tuple-element.6) | data formatting | bytes 524288
  90.5 1.5 %copy.27 = bf16[64,512]{1,0:T(8,128)(2,1)} copy(bf16[64,512]{1,0:T(8,128)(2,1)} %get-tuple-element.7) | data formatting | bytes 131072
  92.0 1.3 %copy.28 = bf16[64,64]{1,0:T(8,128)(2,1)} copy(bf16[64,64]{1,0:T(8,128)(2,1)} %get-tuple-element.8) | data formatting | bytes 16384

commit v3 on v2

--- a/solution.py
+++ b/solution.py
@@ -62,12 +62,18 @@
     uk_copy.start()
     for i in range(1, 4):
         query_copy(i).start()
+    for n in range(12, 16):
+        cache_copy(n).start()
+    for copy in kr_copies:
+        copy.start()
+    for n in range(8):
+        cache_copy(n).start()
 
     lane = lax.broadcasted_iota(jnp.int32, (rows, lanes), 1)
     hidden_copy.wait()
     hidden = hidden_ref[...].astype(jnp.float32)
     inv = lax.rsqrt(jnp.mean(hidden * hidden, axis=-1, keepdims=True) + NORM_EPS)
-    tokx[0:rows] = (hidden * inv * again_ref[...].astype(jnp.float32)).astype(jnp.bfloat16)
+    tokx[0:rows] = (hidden * inv * again_ref[...].astype(jnp.float32).reshape(1, -1)).astype(jnp.bfloat16)
     for b in range(rows):
         pos[b:b + 1, :] = jnp.full((1, lanes), lens_ref[b], jnp.int32).astype(jnp.float32)
     quarter = lax.rem(lane, rope_dim // 2).astype(jnp.float32)
@@ -90,14 +96,11 @@
         q_cols = jnp.dot(tokx[0:rows], gu_buf[i // 2, i % 2, :, 0:qcols], preferred_element_type=jnp.float32)
         q_cols = q_cols.astype(jnp.bfloat16).astype(jnp.float32)
         if i == 0:
-            for n in range(12, 16):
+            for copy in uv_copies + out_copies:
+                copy.start()
+            for n in range(8, 12):
                 cache_copy(n).start()
-            for copy in kr_copies:
-                copy.start()
             uk_copy.wait()
-        if i == 1:
-            for n in range(4):
-                cache_copy(n).start()
         for pair in range(qcols // (2 * head_dim)):
             base = pair * 2 * head_dim
             tile0, tile1, tile2 = (q_cols[:, base + k * lanes:base + (k + 1) * lanes] for k in range(3))
@@ -109,10 +112,6 @@
                 h = head + odd
                 uk_head = gu_buf[0, 1, h * nope:(h + 1) * nope, cache_cols]
                 qlat[:, row_of(h), :] = jnp.dot(nopes[odd].astype(jnp.bfloat16), uk_head, preferred_element_type=jnp.float32)
-    for n in range(4, 12):
-        cache_copy(n).start()
-    for copy in uv_copies + out_copies:
-        copy.start()
     hooks[0]()
 
     for copy in latent_copies:
@@ -122,7 +121,7 @@
     part1 = lax.dot_general(tokx[0:rows], dn_buf[2, four:four + lat1], contract, preferred_element_type=jnp.float32)
     latent = jnp.concatenate([part0, part1[:, :lora - lat0]], axis=-1)
     inv = lax.rsqrt(jnp.mean(latent * latent, axis=-1, keepdims=True) + NORM_EPS)
-    c_new = (latent * inv * kgain_ref[...].astype(jnp.float32)).astype(jnp.bfloat16)
+    c_new = (latent * inv * kgain_ref[...].astype(jnp.float32).reshape(1, -1)).astype(jnp.bfloat16)
     cnew_ref[...] = c_new
     newc[...] = c_new.astype(jnp.float32)
     key_part = jnp.concatenate([part1[:, lora - lat0:], jnp.zeros((rows, lanes - rope_dim), jnp.float32)], axis=-1)
@@ -299,7 +298,7 @@
 
     resid = resid.astype(jnp.float32)
     inv = lax.rsqrt(jnp.mean(resid * resid, axis=-1, keepdims=True) + NORM_EPS)
-    u = (resid * inv * gain_ref[...].astype(jnp.float32)).astype(jnp.bfloat16)
+    u = (resid * inv * gain_ref[...].astype(jnp.float32).reshape(1, -1)).astype(jnp.bfloat16)
     expert_i = lax.broadcasted_iota(jnp.int32, (lanes, rows), 0)
     picked = ids_ref[0:1, :] == expert_i
     for k in range(1, top_k):
@@ -314,6 +313,28 @@
     for h in range(2):
         ublk[me, h, :, :width] = u[h * half:(h + 1) * half]
         ublk[me, h, :, width:] = codes[h * half:(h + 1) * half]
+    pl.semaphore_wait(barrier, group - 1)
+
+    def block_copy(block, h, dest, sem_no):
+        return pltpu.make_async_remote_copy(src_ref=ublk.at[block, h], dst_ref=ublk.at[block, h], send_sem=us_sem.at[sem_no], recv_sem=ur_sem.at[block, h], device_id={dp_axis: dest}, device_id_type=MESH_ID)
+
+    def crossed(block):
+        return lax.rem(block + 1 - 2 * core + group, group)
+
+    first_sends = ((me, 0, right), (me, 1, left), (me, 1, right), (me, 0, left), (me, 0, partner), (me, 1, partner))
+    relays = ((left, 0, right), (left, 0, partner), (right, 1, left), (right, 1, partner), (left, 1, partner), (right, 0, partner), (far, 0, partner), (far, 1, partner))
+    all_sends = first_sends + relays
+
+    def send_block(n):
+        block, h, dest = all_sends[n]
+        block_copy(block, h, dest, n).start()
+
+    def arrived(block, h):
+        block_copy(block, h, partner, 0).wait_recv()
+
+    for n in range(len(first_sends)):
+        send_block(n)
+
     logits = lax.dot_general(u, router_ref[...], (((1,), (1,)), ((), ())), preferred_element_type=jnp.float32)
     logits = logits - jnp.max(logits, axis=-1, keepdims=True)
     expl = jnp.exp(logits)
@@ -328,28 +349,6 @@
     table[2] = p1
     table[3] = p2
     acc[...] = resid
-
-    pl.semaphore_wait(barrier, group - 1)
-
-    def block_copy(block, h, dest, sem_no):
-        return pltpu.make_async_remote_copy(src_ref=ublk.at[block, h], dst_ref=ublk.at[block, h], send_sem=us_sem.at[sem_no], recv_sem=ur_sem.at[block, h], device_id={dp_axis: dest}, device_id_type=MESH_ID)
-
-    def crossed(block):
-        return lax.rem(block + 1 - 2 * core + group, group)
-
-    first_sends = ((me, 0, right), (me, 1, left), (me, 1, right), (me, 0, left), (me, 0, partner), (me, 1, partner))
-    relays = ((left, 0, right), (left, 0, partner), (right, 1, left), (right, 1, partner), (left, 1, partner), (right, 0, partner), (far, 0, partner), (far, 1, partner))
-    all_sends = first_sends + relays
-
-    def send_block(n):
-        block, h, dest = all_sends[n]
-        block_copy(block, h, dest, n).start()
-
-    def arrived(block, h):
-        block_copy(block, h, partner, 0).wait_recv()
-
-    for n in range(len(first_sends)):
-        send_block(n)
 
     def relay():
         seen = set()
@@ -495,6 +494,11 @@
     lax.fori_loop(0, experts_dev, drain, 0)
 
 
+def hand_on(*refs):
+    for k in range(3):
+        refs[3 + k][...] = refs[k][...]
+
+
 def layer(group, cap, hidden, ckv_cache, kr_cache, seq_lens, expert_ids, attn_gain, kv_gain, moe_gain, w_q, w_dkv, w_uk, w_uv, w_o, w_router, shared_gate, shared_up, shared_down, expert_gate, expert_up, expert_down):
     rows, width = hidden.shape
     heads, nope, lora = w_uk.shape
@@ -507,7 +511,7 @@
     dims = (group, experts_dev, experts, cap, depth, 'dp')
     vmem = pl.BlockSpec(memory_space=pltpu.VMEM)
     hbm = pl.BlockSpec(memory_space=pl.ANY)
-    return pl.pallas_call(
+    results = pl.pallas_call(
         functools.partial(layer_kernel, dims),
         out_shape=(jax.ShapeDtypeStruct((rows, width), jnp.bfloat16), jax.ShapeDtypeStruct((rows, lora), jnp.bfloat16), jax.ShapeDtypeStruct((rows, rope_dim), jnp.bfloat16)),
         in_specs=[hbm, pl.BlockSpec(memory_space=pltpu.SMEM)] + [vmem] * 5 + [hbm] * 13,
@@ -538,9 +542,16 @@
         ],
         compiler_params=pltpu.CompilerParams(collective_id=0, has_side_effects=True, vmem_limit_bytes=67043328),
         name='decoder_layer',
-    )(hidden, seq_lens, expert_ids.T, attn_gain.reshape(1, -1), kv_gain.reshape(1, -1), moe_gain.reshape(1, -1), w_router.T,
+    )(hidden, seq_lens, expert_ids.T, attn_gain, kv_gain, moe_gain, w_router.T,
       ckv_cache.reshape(rows * length, lora), jnp.swapaxes(kr_cache, 1, 2).reshape(rows * rope_dim, length), w_q, w_dkv.T, w_uk.reshape(heads * nope, lora),
       w_uv.reshape(heads // 2, experts_dev, group, 16, -1), w_o, shared_gate, shared_up, shared_down, expert_gate, expert_up, expert_down)
+    return pl.pallas_call(
+        hand_on,
+        out_shape=tuple(jax.ShapeDtypeStruct(r.shape, r.dtype) for r in results),
+        in_specs=[vmem] * 3,
+        out_specs=(vmem,) * 3,
+        name='hand_on',
+    )(*results)
 
 
 def solution(mesh):

time: 93.6 us -> 87.8 us (0.938)
  local copies, waits for them, and re-layouts: 8.3 us -> 0 us
  Pallas kernels: 84.4 us -> 87.1 us
    unnamed x3 -> x0, local copies, waits for them, and re-layouts: 4.46 us -> none
    reshape x3 -> x0, local copies, waits for them, and re-layouts: 3.84 us -> none  [the longest x1 1.29 us: layer(): attn_gain.reshape(1, -1)]
    pallas_call x0 -> x1, Pallas kernels: none -> 1.72 us  [layer(): pl.pallas_call(hand_on, out_shape=tuple((jax.ShapeDtypeStruct(r.shape, r....]
    pallas_call x1, Pallas kernels: 84.4 us -> 85.3 us  [layer(): pl.pallas_call(functools.partial(layer_kernel, dims), out_shape=(jax.Shap...]
where the time goes in v3:
time: 87.8 us; the launch traced here: 87.7 us
  Pallas kernels  87.1 us (99%)
    pallas_call x1, Pallas kernels, layer(): pl.pallas_call(functools.partial(layer_kernel, dims), out_shape=(jax.Shap...  85.3 us

profile of v3, /device:TPU:113, one launch (start us, length us, event | category | flops | bytes accessed | tf_op | source)
XLA Modules:
  0.0 87.7 jit_solution(11204334110165502491)
XLA Ops:
  0.6 85.3 %decoder_layer.1 = (bf16[64,2048]{1,0:T(8,128)(2,1)}, bf16[64,512]{1,0:T(8,128)(2,1)}, bf16[64,64]{1,0:T(8,128)(2,1)}) custom-call(bf16[64,2048]{1,0:T(8,128)(2,1)} %hidden_hbm.1, s32[64]{0:T(128)} %lens_ref.1, s32[6,64]{1,0:T(8,128)} %bitcast.15, bf16[2048]{0:T(1024)(128)(2,1)} %again_ref.1, bf16[512]{0:T(512)(128)(2,1)} %kgain_ref.1, ...), custom_call_target="tpu_custom_call" | custom-call | tf_op jit(solution)/shard_map/decoder_layer/pallas_call | solution.py:514
  86.0 1.7 %hand_on.1 = (bf16[64,2048]{1,0:T(8,128)(2,1)}, bf16[64,512]{1,0:T(8,128)(2,1)}, bf16[64,64]{1,0:T(8,128)(2,1)}) custom-call(bf16[64,2048]{1,0:T(8,128)(2,1)} %get-tuple-element.6.refs_0_, bf16[64,512]{1,0:T(8,128)(2,1)} %get-tuple-element.7.refs_1_, bf16[64,64]{1,0:T(8,128)(2,1)} %get-tuple-element.8.refs_2_), custom_call_target="tpu_custom_call" | custom-call | tf_op jit(solution)/shard_map/hand_on/pallas_call | solution.py:548

commit v4 on v3

--- a/solution.py
+++ b/solution.py
@@ -19,8 +19,10 @@
     (hidden_hbm, hidden_ref, lens_ref, again_ref, kgain_ref, ckv_hbm, krt_hbm, wq_hbm, dkvt_hbm, uk_hbm, uv_hbm, wo_hbm, cnew_ref, knew_ref,
      tokx, uvbuf, gu_buf, dn_buf, qlat, qrot, newc, newk, pos, a_sem, c_sem) = refs
     rows, width = hidden_ref.shape
-    lora = qlat.shape[-1]
-    heads = qlat.shape[1]
+    lanes = 128
+    tiles = qlat.shape[0]
+    lora = tiles * lanes
+    heads = qlat.shape[1] // rows
     rope_dim = krt_hbm.shape[0] // rows
     length = krt_hbm.shape[1]
     nope = uk_hbm.shape[0] // heads
@@ -111,7 +113,9 @@
             for odd in range(2):
                 h = head + odd
                 uk_head = gu_buf[0, 1, h * nope:(h + 1) * nope, cache_cols]
-                qlat[:, row_of(h), :] = jnp.dot(nopes[odd].astype(jnp.bfloat16), uk_head, preferred_element_type=jnp.float32)
+                q_head = jnp.dot(nopes[odd].astype(jnp.bfloat16), uk_head, preferred_element_type=jnp.float32)
+                for j in range(tiles):
+                    qlat[j, pl.ds(row_of(h), rows, stride=heads), :] = q_head[:, j * lanes:(j + 1) * lanes]
     hooks[0]()
 
     for copy in latent_copies:
@@ -135,7 +139,7 @@
         scores, news = [], []
         for s in range(8):
             b = seq0 + s
-            q_b = qlat[b].astype(jnp.bfloat16)
+            q_b = jnp.concatenate([qlat[j, pl.ds(pl.multiple_of(b * heads, heads), heads), :] for j in range(tiles)], axis=-1).astype(jnp.bfloat16)
             pairs = qrot[b]
             r_b = jnp.concatenate([pairs, pltpu.roll(pairs, lanes // 2, 1)], axis=0).astype(jnp.bfloat16)
             score = lax.dot_general(q_b, keys(s), contract, preferred_element_type=jnp.float32)
@@ -155,7 +159,9 @@
         for s in range(8):
             b = seq0 + s
             out = jnp.dot(prob[s * heads:(s + 1) * heads], keys(s), preferred_element_type=jnp.float32)
-            qlat[b] = out + prob_new[s * heads:(s + 1) * heads] * newc[pl.ds(b, 1), :]
+            out += prob_new[s * heads:(s + 1) * heads] * newc[pl.ds(b, 1), :]
+            for j in range(tiles):
+                qlat[j, pl.ds(pl.multiple_of(b * heads, heads), heads), :] = out[:, j * lanes:(j + 1) * lanes]
 
     for copy in kr_copies:
         copy.wait()
@@ -199,7 +205,7 @@
     for copy in uv_copies:
         copy.wait()
     for h in range(heads):
-        o_lat = qlat[:, row_of(h), :].astype(jnp.bfloat16)
+        o_lat = jnp.concatenate([qlat[j, pl.ds(row_of(h), rows, stride=heads), :] for j in range(tiles)], axis=-1).astype(jnp.bfloat16)
         uv_half = uvbuf.shape[0] // 2
         uv_head = uvbuf[(h % 2) * uv_half:(h % 2 + 1) * uv_half, :, :, (h // 2) * value_dim:(h // 2 + 1) * value_dim].reshape(lora, value_dim)
         tokx[rows:2 * rows, h * value_dim:(h + 1) * value_dim] = jnp.dot(o_lat, uv_head, preferred_element_type=jnp.float32).astype(jnp.bfloat16)
@@ -527,7 +533,7 @@
             pltpu.VMEM((slots, width - main), jnp.float32),
             pltpu.VMEM((depth, 2, width, ff), jnp.bfloat16),
             pltpu.VMEM((depth, ff, width), jnp.bfloat16),
-            pltpu.VMEM((rows, heads, lora), jnp.float32),
+            pltpu.VMEM((lora // 128, rows * heads, 128), jnp.float32),
             pltpu.VMEM((rows, heads // 2, 128), jnp.float32),
             pltpu.VMEM((rows, lora), jnp.float32),
             pltpu.VMEM((rows, 128), jnp.float32),

time: 87.8 us -> 86.8 us (0.989)
  Pallas kernels: 87.1 us -> 86 us
    pallas_call x1, Pallas kernels: 85.3 us -> 84.3 us  [layer(): pl.pallas_call(functools.partial(layer_kernel, dims), out_shape=(jax.Shap...]
where the time goes in v4:
time: 86.8 us; the launch traced here: 86.6 us
  Pallas kernels  86 us (99%)
    pallas_call x1, Pallas kernels, layer(): pl.pallas_call(functools.partial(layer_kernel, dims), out_shape=(jax.Shap...  84.3 us

profile of v4, /device:TPU:113, one launch (start us, length us, event | category | flops | bytes accessed | tf_op | source)
XLA Modules:
  0.0 86.6 jit_solution(7194588228583372762)
XLA Ops:
  0.6 84.3 %decoder_layer.1 = (bf16[64,2048]{1,0:T(8,128)(2,1)}, bf16[64,512]{1,0:T(8,128)(2,1)}, bf16[64,64]{1,0:T(8,128)(2,1)}) custom-call(bf16[64,2048]{1,0:T(8,128)(2,1)} %hidden_hbm.1, s32[64]{0:T(128)} %lens_ref.1, s32[6,64]{1,0:T(8,128)} %bitcast.15, bf16[2048]{0:T(1024)(128)(2,1)} %again_ref.1, bf16[512]{0:T(512)(128)(2,1)} %kgain_ref.1, ...), custom_call_target="tpu_custom_call" | custom-call | tf_op jit(solution)/shard_map/decoder_layer/pallas_call | solution.py:520
  84.9 1.7 %hand_on.1 = (bf16[64,2048]{1,0:T(8,128)(2,1)}, bf16[64,512]{1,0:T(8,128)(2,1)}, bf16[64,64]{1,0:T(8,128)(2,1)}) custom-call(bf16[64,2048]{1,0:T(8,128)(2,1)} %get-tuple-element.6.refs_0_, bf16[64,512]{1,0:T(8,128)(2,1)} %get-tuple-element.7.refs_1_, bf16[64,64]{1,0:T(8,128)(2,1)} %get-tuple-element.8.refs_2_), custom_call_target="tpu_custom_call" | custom-call | tf_op jit(solution)/shard_map/hand_on/pallas_call | solution.py:554

commit v5 on v4

--- a/solution.py
+++ b/solution.py
@@ -98,10 +98,10 @@
         q_cols = jnp.dot(tokx[0:rows], gu_buf[i // 2, i % 2, :, 0:qcols], preferred_element_type=jnp.float32)
         q_cols = q_cols.astype(jnp.bfloat16).astype(jnp.float32)
         if i == 0:
+            for n in range(8, 12):
+                cache_copy(n).start()
             for copy in uv_copies + out_copies:
                 copy.start()
-            for n in range(8, 12):
-                cache_copy(n).start()
             uk_copy.wait()
         for pair in range(qcols // (2 * head_dim)):
             base = pair * 2 * head_dim
@@ -251,6 +251,9 @@
     def routed(step):
         return (step >= 1) & (step <= experts_dev)
 
+    def act(copy, action):
+        getattr(copy, action)()
+
     def either(condition, action_a, action_b):
         if isinstance(condition, bool):
             (action_a if condition else action_b)()
@@ -271,16 +274,17 @@
 
         either(routed(step), own, shared)
 
-    def weights_dn(step, action):
+    def weights_dn(step, action, part=None):
         slot = step % depth if isinstance(step, int) else lax.rem(step, depth)
+        first, count = (0, ff) if part is None else (part * (ff // 2), ff // 2)
 
         def own():
-            getattr(pltpu.make_async_copy(edown_hbm.at[step - 1], dn_buf.at[slot], dn_sem.at[slot]), action)()
+            act(pltpu.make_async_copy(edown_hbm.at[step - 1, first:first + count], dn_buf.at[slot, first:first + count], dn_sem.at[slot]), action)
 
         def shared():
-            start = step // (steps - 1) * ff
-            cols = pl.ds(start if isinstance(step, int) else pl.multiple_of(start, 128), ff)
-            getattr(pltpu.make_async_copy(sdown_hbm.at[cols], dn_buf.at[slot], dn_sem.at[slot]), action)()
+            start = step // (steps - 1) * ff + first
+            cols = pl.ds(start if isinstance(step, int) else pl.multiple_of(start, 64), count)
+            act(pltpu.make_async_copy(sdown_hbm.at[cols], dn_buf.at[slot, first:first + count], dn_sem.at[slot]), action)
 
         either(routed(step), own, shared)
 
@@ -293,12 +297,22 @@
         pl.semaphore_signal(barrier, inc=1, device_id={dp_axis: lax.rem(me + k, group)}, device_id_type=MESH_ID)
 
     def freed_deep(it):
-        for d in range(depth):
-            @pl.when(it == 2 * d + 1)
-            def _():
-                weights_dn(d, "start")
-
-    hooks = (lambda: fetch(0), lambda: fetch(1), freed_deep, lambda: fetch(2))
+        @pl.when(it == 3)
+        def _():
+            fetch(0)
+
+        @pl.when(it == 4)
+        def _():
+            weights_dn(0, "start")
+
+        @pl.when(it == 5)
+        def _():
+            weights_gu(1, 0, egate_hbm, sgate_hbm, "start")
+
+    def nothing():
+        pass
+
+    hooks = (nothing, nothing, freed_deep, nothing)
     resid = attention_phase((hidden_hbm, out_ref, lens_ref, again_ref, kgain_ref, ckv_hbm, krt_hbm, wq_hbm, dkvt_hbm, uk_hbm, uv_hbm, wo_hbm, cnew_ref, knew_ref,
                              tokx, send, gu_buf, dn_buf, qlat, qrot, newc, newk, acc.at[:, 0:128], a_sem, c_sem), hooks)
 
@@ -327,9 +341,9 @@
     def crossed(block):
         return lax.rem(block + 1 - 2 * core + group, group)
 
-    first_sends = ((me, 0, right), (me, 1, left), (me, 1, right), (me, 0, left), (me, 0, partner), (me, 1, partner))
-    relays = ((left, 0, right), (left, 0, partner), (right, 1, left), (right, 1, partner), (left, 1, partner), (right, 0, partner), (far, 0, partner), (far, 1, partner))
-    all_sends = first_sends + relays
+    all_sends = ((me, 0, right), (me, 1, left), (me, 1, right), (me, 0, left), (me, 0, partner), (me, 1, partner),
+                 (left, 0, right), (right, 1, left), (left, 0, partner), (right, 1, partner),
+                 (left, 1, partner), (right, 0, partner), (far, 0, partner), (far, 1, partner))
 
     def send_block(n):
         block, h, dest = all_sends[n]
@@ -338,8 +352,39 @@
     def arrived(block, h):
         block_copy(block, h, partner, 0).wait_recv()
 
-    for n in range(len(first_sends)):
+    for n in (0, 1, 4, 5):
         send_block(n)
+    weights_gu(1, 1, eup_hbm, sup_hbm, "start")
+    weights_dn(1, "start")
+    for n in (2, 3):
+        send_block(n)
+
+    def first_relay():
+        arrived(left, 0)
+        send_block(8)
+        arrived(right, 1)
+        send_block(9)
+        weights_gu(2, 0, egate_hbm, sgate_hbm, "start")
+        send_block(6)
+        send_block(7)
+        weights_gu(2, 1, eup_hbm, sup_hbm, "start")
+
+    def relay():
+        arrived(left, 1)
+        send_block(10)
+        arrived(right, 0)
+        send_block(11)
+        weights_dn(2, "start")
+        weights_gu(3, 0, egate_hbm, sgate_hbm, "start")
+        arrived(far, 0)
+        send_block(12)
+        arrived(far, 1)
+        send_block(13)
+        weights_gu(3, 1, eup_hbm, sup_hbm, "start")
+        weights_dn(3, "start")
+        for block in (partner, crossed(left), crossed(right), crossed(far)):
+            for h in range(2):
+                arrived(block, h)
 
     logits = lax.dot_general(u, router_ref[...], (((1,), (1,)), ((), ())), preferred_element_type=jnp.float32)
     logits = logits - jnp.max(logits, axis=-1, keepdims=True)
@@ -356,18 +401,6 @@
     table[3] = p2
     acc[...] = resid
 
-    def relay():
-        seen = set()
-        for n in range(len(first_sends), len(all_sends)):
-            block, h, _ = all_sends[n]
-            if (id(block), h) not in seen:
-                seen.add((id(block), h))
-                arrived(block, h)
-            send_block(n)
-        for block in (partner, crossed(left), crossed(right), crossed(far)):
-            for h in range(2):
-                arrived(block, h)
-
     row_i = lax.broadcasted_iota(jnp.int32, (lanes, slots), 0)
     col_i = lax.broadcasted_iota(jnp.int32, (lanes, slots), 1)
 
@@ -376,6 +409,12 @@
 
     def arrival(step, source):
         return pltpu.make_async_remote_copy(src_ref=send.at[step, source], dst_ref=recv.at[step, source], send_sem=ys_sem.at[step, source], recv_sem=yr_sem.at[step, source], device_id={dp_axis: source}, device_id_type=MESH_ID)
+
+    groups = ((far, partner), (right, left), (crossed(far),), (crossed(right), crossed(left)))
+
+    def send_group(step, n):
+        for dest in groups[n]:
+            return_copy(step, dest).start()
 
     def gather_rows(expert):
         pick = (row_i == me * experts_dev + expert).astype(jnp.float32).astype(jnp.bfloat16)
@@ -442,9 +481,24 @@
             up_act = jnp.dot(tokx[...], gu_buf[slot, 1, :, c0:c1], preferred_element_type=jnp.float32)
             midx[:, c0:c1] = (silu(gate_act) * up_act).astype(jnp.bfloat16)
 
-        @pl.when(step + depth < steps)
-        def _():
-            fetch(step + depth)
+        more = (step >= 1) & (step + depth < steps)
+        second = (step >= 2) & (step + depth <= steps)
+
+        @pl.when(more)
+        def _():
+            weights_gu(step + depth, 0, egate_hbm, sgate_hbm, "start")
+
+        @pl.when(second)
+        def _():
+            send_group(expert - 1, 2)
+
+        @pl.when(more)
+        def _():
+            weights_gu(step + depth, 1, eup_hbm, sup_hbm, "start")
+
+        @pl.when(second)
+        def _():
+            send_group(expert - 1, 3)
 
         weights_dn(step, "wait")
         tail[...] = jnp.dot(midx[...], dn_buf[slot, :, main:], preferred_element_type=jnp.float32)
@@ -464,15 +518,25 @@
             def _():
                 acc[:, q * blk:(q + 1) * blk] += y_main[:rows]
 
-        @pl.when(step + depth < steps)
-        def _():
-            weights_dn(step + depth, "start")
-
         @pl.when(is_routed)
         def _():
             recv[expert, me] = send[expert, me]
-            for k in (4, 3, 5, 2, 6, 1, 7):
-                return_copy(expert, lax.rem(me + k, group)).start()
+
+        @pl.when(more)
+        def _():
+            weights_dn(step + depth, "start", 0)
+            send_group(expert, 0)
+            weights_dn(step + depth, "start", 1)
+            send_group(expert, 1)
+
+        @pl.when(is_routed & jnp.logical_not(more))
+        def _():
+            for n in range(4):
+                send_group(expert, n)
+
+        @pl.when(step == 0)
+        def _():
+            first_relay()
 
         @pl.when(expert >= lag)
         def _():

time: 86.8 us -> 87 us (level)
  no operation moved by 1% of the time
where the time goes in v5:
time: 87 us; the launch traced here: 86.9 us
  Pallas kernels  86.2 us (99%)
    pallas_call x1, Pallas kernels, layer(): pl.pallas_call(functools.partial(layer_kernel, dims), out_shape=(jax.Shap...  84.5 us

profile of v5, /device:TPU:113, one launch (start us, length us, event | category | flops | bytes accessed | tf_op | source)
XLA Modules:
  0.0 86.9 jit_solution(9473738143295053045)
XLA Ops:
  0.6 84.5 %decoder_layer.1 = (bf16[64,2048]{1,0:T(8,128)(2,1)}, bf16[64,512]{1,0:T(8,128)(2,1)}, bf16[64,64]{1,0:T(8,128)(2,1)}) custom-call(bf16[64,2048]{1,0:T(8,128)(2,1)} %hidden_hbm.1, s32[64]{0:T(128)} %lens_ref.1, s32[6,64]{1,0:T(8,128)} %bitcast.15, bf16[2048]{0:T(1024)(128)(2,1)} %again_ref.1, bf16[512]{0:T(512)(128)(2,1)} %kgain_ref.1, ...), custom_call_target="tpu_custom_call" | custom-call | tf_op jit(solution)/shard_map/decoder_layer/pallas_call | solution.py:584
  85.1 1.7 %hand_on.1 = (bf16[64,2048]{1,0:T(8,128)(2,1)}, bf16[64,512]{1,0:T(8,128)(2,1)}, bf16[64,64]{1,0:T(8,128)(2,1)}) custom-call(bf16[64,2048]{1,0:T(8,128)(2,1)} %get-tuple-element.6.refs_0_, bf16[64,512]{1,0:T(8,128)(2,1)} %get-tuple-element.7.refs_1_, bf16[64,64]{1,0:T(8,128)(2,1)} %get-tuple-element.8.refs_2_), custom_call_target="tpu_custom_call" | custom-call | tf_op jit(solution)/shard_map/hand_on/pallas_call | solution.py:618

commit v6 on v4

--- a/solution.py
+++ b/solution.py
@@ -58,6 +58,7 @@
 
     hidden_copy = pltpu.make_async_copy(hidden_hbm, hidden_ref, a_sem.at[19])
     hidden_copy.start()
+    hooks[5]()
     query_copy(0).start()
     for copy in latent_copies:
         copy.start()
@@ -70,6 +71,8 @@
         copy.start()
     for n in range(8):
         cache_copy(n).start()
+
+    hooks[4]()
 
     lane = lax.broadcasted_iota(jnp.int32, (rows, lanes), 1)
     hidden_copy.wait()
@@ -222,9 +225,10 @@
     return value * (1.0 / (1.0 + jnp.exp(-value)))
 
 
-def layer_kernel(dims, hidden_hbm, lens_ref, ids_ref, again_ref, kgain_ref, gain_ref, router_ref, ckv_hbm, krt_hbm, wq_hbm, dkvt_hbm, uk_hbm, uv_hbm, wo_hbm,
+def layer_kernel(dims, hidden_hbm, lens_hbm, ids_hbm, again_hbm, kgain_hbm, gain_hbm, router_hbm, ckv_hbm, krt_hbm, wq_hbm, dkvt_hbm, uk_hbm, uv_hbm, wo_hbm,
                  sgate_hbm, sup_hbm, sdown_hbm, egate_hbm, eup_hbm, edown_hbm, out_ref, cnew_ref, knew_ref,
                  ublk, tokx, midx, send, recv, acc, table, tail, gu_buf, dn_buf, qlat, qrot, newc, newk,
+                 lens_ref, ids_ref, again_ref, kgain_ref, gain_ref, router_ref, small_sem,
                  gu_sem, dn_sem, us_sem, ur_sem, ys_sem, yr_sem, a_sem, c_sem):
     group, experts_dev, experts, cap, depth, dp_axis = dims
     rows, width = hidden_hbm.shape
@@ -236,7 +240,7 @@
     slots = group * slot16
     main = send.shape[-1]
     blk = main // 3
-    top_k = ids_ref.shape[0]
+    top_k = ids_hbm.shape[0]
     lag = 4
     lanes = 128
     me = lax.axis_index(dp_axis)
@@ -289,8 +293,33 @@
         weights_gu(step, 1, eup_hbm, sup_hbm, "start")
 
     barrier = pltpu.get_barrier_semaphore()
-    for k in range(1, group):
-        pl.semaphore_signal(barrier, inc=1, device_id={dp_axis: lax.rem(me + k, group)}, device_id_type=MESH_ID)
+    small = [pltpu.make_async_copy(src, dst, small_sem.at[k]) for k, (src, dst) in enumerate(
+        ((again_hbm, again_ref), (lens_hbm, lens_ref), (ids_hbm, ids_ref), (kgain_hbm, kgain_ref), (gain_hbm, gain_ref), (router_hbm, router_ref)))]
+
+    def request():
+        for copy in small:
+            copy.start()
+
+    def opening():
+        for k in range(1, group):
+            pl.semaphore_signal(barrier, inc=1, device_id={dp_axis: lax.rem(me + k, group)}, device_id_type=MESH_ID)
+        small[2].wait()
+        expert_i = lax.broadcasted_iota(jnp.int32, (lanes, rows), 0)
+        picked = ids_ref[0:1, :] == expert_i
+        for k in range(1, top_k):
+            picked = picked | (ids_ref[k:k + 1, :] == expert_i)
+        tok_a = lax.broadcasted_iota(jnp.int32, (rows, rows), 0)
+        tok_b = lax.broadcasted_iota(jnp.int32, (rows, rows), 1)
+        before = jnp.where(tok_a < tok_b, 1.0, 0.0).astype(jnp.bfloat16)
+        rank = jnp.dot(jnp.where(picked, 1.0, 0.0).astype(jnp.bfloat16), before, preferred_element_type=jnp.float32)
+        codes_t = jnp.where(picked, rank, -1.0).astype(jnp.bfloat16)
+        same = jnp.where(tok_a == tok_b, 1.0, 0.0).astype(jnp.bfloat16)
+        codes = lax.dot_general(same, codes_t, (((1,), (1,)), ((), ())), preferred_element_type=jnp.float32).astype(jnp.bfloat16)
+        table[0] = codes
+        for h in range(2):
+            ublk[me, h, :, width:] = codes[h * half:(h + 1) * half]
+        for k in (0, 1, 3, 4, 5):
+            small[k].wait()
 
     def freed_deep(it):
         for d in range(depth):
@@ -298,27 +327,15 @@
             def _():
                 weights_dn(d, "start")
 
-    hooks = (lambda: fetch(0), lambda: fetch(1), freed_deep, lambda: fetch(2))
+    hooks = (lambda: fetch(0), lambda: fetch(1), freed_deep, lambda: fetch(2), opening, request)
     resid = attention_phase((hidden_hbm, out_ref, lens_ref, again_ref, kgain_ref, ckv_hbm, krt_hbm, wq_hbm, dkvt_hbm, uk_hbm, uv_hbm, wo_hbm, cnew_ref, knew_ref,
                              tokx, send, gu_buf, dn_buf, qlat, qrot, newc, newk, acc.at[:, 0:128], a_sem, c_sem), hooks)
 
     resid = resid.astype(jnp.float32)
     inv = lax.rsqrt(jnp.mean(resid * resid, axis=-1, keepdims=True) + NORM_EPS)
     u = (resid * inv * gain_ref[...].astype(jnp.float32).reshape(1, -1)).astype(jnp.bfloat16)
-    expert_i = lax.broadcasted_iota(jnp.int32, (lanes, rows), 0)
-    picked = ids_ref[0:1, :] == expert_i
-    for k in range(1, top_k):
-        picked = picked | (ids_ref[k:k + 1, :] == expert_i)
-    tok_a = lax.broadcasted_iota(jnp.int32, (rows, rows), 0)
-    tok_b = lax.broadcasted_iota(jnp.int32, (rows, rows), 1)
-    before = jnp.where(tok_a < tok_b, 1.0, 0.0).astype(jnp.bfloat16)
-    rank = jnp.dot(jnp.where(picked, 1.0, 0.0).astype(jnp.bfloat16), before, preferred_element_type=jnp.float32)
-    codes_t = jnp.where(picked, rank, -1.0).astype(jnp.bfloat16)
-    same = jnp.where(tok_a == tok_b, 1.0, 0.0).astype(jnp.bfloat16)
-    codes = lax.dot_general(same, codes_t, (((1,), (1,)), ((), ())), preferred_element_type=jnp.float32).astype(jnp.bfloat16)
     for h in range(2):
         ublk[me, h, :, :width] = u[h * half:(h + 1) * half]
-        ublk[me, h, :, width:] = codes[h * half:(h + 1) * half]
     pl.semaphore_wait(barrier, group - 1)
 
     def block_copy(block, h, dest, sem_no):
@@ -350,7 +367,6 @@
     rest = prob - p0.astype(jnp.float32)
     p1 = rest.astype(jnp.bfloat16)
     p2 = (rest - p1.astype(jnp.float32)).astype(jnp.bfloat16)
-    table[0] = codes
     table[1] = p0
     table[2] = p1
     table[3] = p2
@@ -520,7 +536,7 @@
     results = pl.pallas_call(
         functools.partial(layer_kernel, dims),
         out_shape=(jax.ShapeDtypeStruct((rows, width), jnp.bfloat16), jax.ShapeDtypeStruct((rows, lora), jnp.bfloat16), jax.ShapeDtypeStruct((rows, rope_dim), jnp.bfloat16)),
-        in_specs=[hbm, pl.BlockSpec(memory_space=pltpu.SMEM)] + [vmem] * 5 + [hbm] * 13,
+        in_specs=[hbm] * 20,
         out_specs=(vmem, vmem, vmem),
         scratch_shapes=[
             pltpu.VMEM((group, 2, rows // 2, width + 128), jnp.bfloat16),
@@ -537,6 +553,13 @@
             pltpu.VMEM((rows, heads // 2, 128), jnp.float32),
             pltpu.VMEM((rows, lora), jnp.float32),
             pltpu.VMEM((rows, 128), jnp.float32),
+            pltpu.SMEM(seq_lens.shape, jnp.int32),
+            pltpu.VMEM(expert_ids.shape[::-1], jnp.int32),
+            pltpu.VMEM(attn_gain.shape, jnp.bfloat16),
+            pltpu.VMEM(kv_gain.shape, jnp.bfloat16),
+            pltpu.VMEM(moe_gain.shape, jnp.bfloat16),
+            pltpu.VMEM(w_router.shape[::-1], jnp.bfloat16),
+            pltpu.SemaphoreType.DMA((6,)),
             pltpu.SemaphoreType.DMA((depth, 2)),
             pltpu.SemaphoreType.DMA((depth,)),
             pltpu.SemaphoreType.DMA((14,)),

time: 86.8 us -> 91.7 us (1.056)
  Pallas kernels: 86 us -> 91 us
    pallas_call x1, Pallas kernels: 84.3 us -> 89.3 us  [layer(): pl.pallas_call(functools.partial(layer_kernel, dims), out_shape=(jax.Shap...]
where the time goes in v6:
time: 91.7 us; the launch traced here: 91.6 us
  Pallas kernels  91 us (99%)
    pallas_call x1, Pallas kernels, layer(): pl.pallas_call(functools.partial(layer_kernel, dims), out_shape=(jax.Shap...  89.3 us

profile of v6, /device:TPU:113, one launch (start us, length us, event | category | flops | bytes accessed | tf_op | source)
XLA Modules:
  0.0 91.6 jit_solution(13879218905238570203)
XLA Ops:
  0.6 89.3 %decoder_layer.1 = (bf16[64,2048]{1,0:T(8,128)(2,1)}, bf16[64,512]{1,0:T(8,128)(2,1)}, bf16[64,64]{1,0:T(8,128)(2,1)}) custom-call(bf16[64,2048]{1,0:T(8,128)(2,1)} %hidden_hbm.1, s32[64]{0:T(128)} %lens_hbm.1, s32[6,64]{1,0:T(8,128)} %bitcast.15, bf16[2048]{0:T(1024)(128)(2,1)} %again_hbm.1, bf16[512]{0:T(512)(128)(2,1)} %kgain_hbm.1, ...), custom_call_target="tpu_custom_call" | custom-call | tf_op jit(solution)/shard_map/decoder_layer/pallas_call | solution.py:536
  89.9 1.7 %hand_on.1 = (bf16[64,2048]{1,0:T(8,128)(2,1)}, bf16[64,512]{1,0:T(8,128)(2,1)}, bf16[64,64]{1,0:T(8,128)(2,1)}) custom-call(bf16[64,2048]{1,0:T(8,128)(2,1)} %get-tuple-element.6.refs_0_, bf16[64,512]{1,0:T(8,128)(2,1)} %get-tuple-element.7.refs_1_, bf16[64,64]{1,0:T(8,128)(2,1)} %get-tuple-element.8.refs_2_), custom_call_target="tpu_custom_call" | custom-call | tf_op jit(solution)/shard_map/hand_on/pallas_call | solution.py:577
